TPU v7x, 16 devices: a whole 2x2x2 slice. The times are simulated.
16 devices in a mesh: sp: 16 (over z, y, x, core).
Axes of the slice: x: 2, y: 2, z: 2, core: 2. Of those that a mesh axis runs over, the one named last changes fastest.
Arguments:
- x: bfloat16 [4, 2048, 1024], P(None, 'sp')
- d_y: bfloat16 [4, 2048, 1024], P(None, 'sp')
- ln_gamma: bfloat16 [1024], replicated
- ln_beta: bfloat16 [1024], replicated
- w_qkv: bfloat16 [1024, 3072], replicated
- b_qkv: bfloat16 [3072], replicated
- w_out: bfloat16 [1024, 1024], replicated
- b_out: bfloat16 [1024], replicated
- head_kind: int32 [16], replicated
Outputs:
- output 1: bfloat16 [4, 2048, 1024], P(None, 'sp')
- output 2: bfloat16 [4, 2048, 1024], P(None, 'sp')
- output 3: float32 [1024], replicated
- output 4: float32 [1024], replicated
- output 5: float32 [1024, 3072], replicated
- output 6: float32 [3072], replicated
- output 7: float32 [1024, 1024], replicated
- output 8: float32 [1024], replicated
All inputs are finite; a program needn't handle non-finite values.
Results may differ from a plain program's by a relative error of at most 0.0134294.
Values are sent between devices in bfloat16 or wider.
A program may use at most 1 GiB of HBM per device.

v0:
```python
import math
import jax
import jax.numpy as jnp
from jax import lax
from jax.sharding import PartitionSpec as P

LN_EPS = 1e-5
NEG_BIG = -1e30


def layer_norm(x_rows, gamma_f, beta_f):
    row_mean = jnp.mean(x_rows, axis=-1, keepdims=True)
    centred = x_rows - row_mean
    row_var = jnp.mean(centred * centred, axis=-1, keepdims=True)
    return centred * lax.rsqrt(row_var + LN_EPS) * gamma_f + beta_f


def score_probs(q_part, k_all, banded, q_first, band_width):
    q_len = q_part.shape[2]
    k_len = k_all.shape[2]
    score_scale = 1.0 / math.sqrt(q_part.shape[3])
    logits = jnp.einsum("bhqd,bhkd->bhqk", q_part, k_all, preferred_element_type=jnp.float32) * score_scale
    query_pos = q_first + lax.broadcasted_iota(jnp.int32, (1, 1, q_len, 1), 2)
    key_pos = lax.broadcasted_iota(jnp.int32, (1, 1, 1, k_len), 3)
    is_banded = (banded == 1)[None, :, None, None]
    allowed = (key_pos <= query_pos) & (jnp.logical_not(is_banded) | (key_pos > query_pos - band_width))
    return jax.nn.softmax(jnp.where(allowed, logits, NEG_BIG), axis=-1)


def attend_forward(q_all, k_all, v_all, banded, q_offset, band_width):
    q_len = q_all.shape[2]
    q_blk = min(128, q_len)

    def q_step(blk_index, out_buf):
        q_start = blk_index * q_blk
        q_part = lax.dynamic_slice_in_dim(q_all, q_start, q_blk, axis=2)
        attn_prob = score_probs(q_part, k_all, banded, q_offset + q_start, band_width)
        o_part = jnp.einsum("bhqk,bhkd->bhqd", attn_prob.astype(jnp.bfloat16), v_all, preferred_element_type=jnp.float32)
        return lax.dynamic_update_slice_in_dim(out_buf, o_part.astype(jnp.bfloat16), q_start, axis=2)

    return lax.fori_loop(0, q_len // q_blk, q_step, jnp.zeros_like(q_all))


def attend_backward(q_all, k_all, v_all, d_out, banded, q_offset, band_width):
    q_len = q_all.shape[2]
    q_blk = min(128, q_len)
    score_scale = 1.0 / math.sqrt(q_all.shape[3])

    def q_step(blk_index, grad_state):
        dq_buf, dk_acc, dv_acc = grad_state
        q_start = blk_index * q_blk
        q_part = lax.dynamic_slice_in_dim(q_all, q_start, q_blk, axis=2)
        do_part = lax.dynamic_slice_in_dim(d_out, q_start, q_blk, axis=2)
        attn_prob = score_probs(q_part, k_all, banded, q_offset + q_start, band_width)
        prob_bf = attn_prob.astype(jnp.bfloat16)
        d_prob = jnp.einsum("bhqd,bhkd->bhqk", do_part, v_all, preferred_element_type=jnp.float32).astype(jnp.bfloat16).astype(jnp.float32)
        d_logit = (attn_prob * (d_prob - jnp.sum(attn_prob * d_prob, axis=-1, keepdims=True)) * score_scale).astype(jnp.bfloat16)
        dq_part = jnp.einsum("bhqk,bhkd->bhqd", d_logit, k_all, preferred_element_type=jnp.float32)
        dk_acc = dk_acc + jnp.einsum("bhqk,bhqd->bhkd", d_logit, q_part, preferred_element_type=jnp.float32)
        dv_acc = dv_acc + jnp.einsum("bhqk,bhqd->bhkd", prob_bf, do_part, preferred_element_type=jnp.float32)
        dq_buf = lax.dynamic_update_slice_in_dim(dq_buf, dq_part.astype(jnp.bfloat16), q_start, axis=2)
        return dq_buf, dk_acc, dv_acc

    init_state = (jnp.zeros_like(q_all), jnp.zeros(k_all.shape, jnp.float32), jnp.zeros(v_all.shape, jnp.float32))
    return lax.fori_loop(0, q_len // q_blk, q_step, init_state)


def solution(mesh):
    seq_par = mesh.shape["sp"]
    tok_spec = P(None, "sp", None)

    def local_block(x, d_y, ln_gamma, ln_beta, w_qkv, b_qkv, w_out, b_out, head_kind):
        local_len = x.shape[1]
        d_model = x.shape[2]
        num_heads = head_kind.shape[0]
        head_dim = d_model // num_heads
        local_heads = num_heads // seq_par
        band_width = local_len * seq_par // 4
        my_kinds = lax.dynamic_slice_in_dim(head_kind, lax.axis_index("sp") * local_heads, local_heads)
        wqkv_r = w_qkv.reshape(d_model, 3, num_heads, head_dim)
        wout_r = w_out.reshape(num_heads, head_dim, d_model)
        x_f = x.astype(jnp.float32)
        h_f, ln_pull = jax.vjp(layer_norm, x_f, ln_gamma.astype(jnp.float32), ln_beta.astype(jnp.float32))
        h_norm = h_f.astype(jnp.bfloat16)
        qkv_bias = b_qkv.astype(jnp.float32).reshape(3, 1, num_heads, 1, head_dim)
        qkv_tok = (jnp.einsum("bsi,itnd->tbnsd", h_norm, wqkv_r, preferred_element_type=jnp.float32) + qkv_bias).astype(jnp.bfloat16)
        qkv_head = lax.all_to_all(qkv_tok, "sp", 2, 3, tiled=True)
        attn_head = attend_forward(qkv_head[0], qkv_head[1], qkv_head[2], my_kinds, 0, band_width)
        attn_tok = lax.all_to_all(attn_head, "sp", 2, 1, tiled=True)
        proj_out = jnp.einsum("bnsd,ndj->bsj", attn_tok, wout_r, preferred_element_type=jnp.float32)
        y_out = (x_f + proj_out + b_out.astype(jnp.float32)).astype(jnp.bfloat16)
        d_attn_tok = jnp.einsum("bsj,ndj->bnsd", d_y, wout_r, preferred_element_type=jnp.float32).astype(jnp.bfloat16)
        d_attn_head = lax.all_to_all(d_attn_tok, "sp", 1, 2, tiled=True)
        dq_head, dk_head, dv_head = attend_backward(qkv_head[0], qkv_head[1], qkv_head[2], d_attn_head, my_kinds, 0, band_width)
        d_qkv_head = jnp.stack([dq_head, dk_head.astype(jnp.bfloat16), dv_head.astype(jnp.bfloat16)])
        d_qkv_tok = lax.all_to_all(d_qkv_head, "sp", 3, 2, tiled=True)
        d_wqkv = jnp.einsum("bsi,tbnsd->itnd", h_norm, d_qkv_tok, preferred_element_type=jnp.float32).reshape(d_model, 3 * d_model)
        d_bqkv = jnp.sum(d_qkv_tok, axis=(1, 3), dtype=jnp.float32).reshape(3 * d_model)
        d_h = jnp.einsum("tbnsd,itnd->bsi", d_qkv_tok, wqkv_r, preferred_element_type=jnp.float32).astype(jnp.bfloat16).astype(jnp.float32)
        d_x_ln, d_gamma, d_beta = ln_pull(d_h)
        d_x = (d_y.astype(jnp.float32) + d_x_ln).astype(jnp.bfloat16)
        d_wout = jnp.einsum("bnsd,bsj->ndj", attn_tok, d_y, preferred_element_type=jnp.float32).reshape(d_model, d_model)
        d_bout = jnp.sum(d_y, axis=(0, 1), dtype=jnp.float32)
        grad_sums = lax.psum((d_gamma, d_beta, d_wqkv, d_bqkv, d_wout, d_bout), "sp")
        return (y_out, d_x) + tuple(grad_sums)

    return jax.shard_map(local_block, mesh=mesh, in_specs=(tok_spec, tok_spec, P(), P(), P(), P(), P(), P(), P()), out_specs=(tok_spec, tok_spec, P(), P(), P(), P(), P(), P()), check_vma=False)
```

profile of v0, /device:TPU:0, one launch (start us, length us, event | category | flops | bytes accessed | tf_op | source)
XLA Modules:
  0.0 967.8 jit_solution(17710025870150648017)
XLA Ops:
  18.0 8.7 copy.86
  47.1 33.6 %all-to-all-done = bf16[3,4,16,128,64]{3,4,0,1,2:T(8,128)(2,1)S(1)} async-done(((bf16[3,4,16,128,64]{3,4,0,1,2:T(8,128)(2,1)}), bf16[3,4,16,128,64]{3,4,0,1,2:T(8,128)(2,1)S(1)}, u32[]{:S(2)}, u32[]{:S(2)}) %all-to-all-start) | async-done | bytes 3145760 | tf_op jit(solution)/shard_map/all_to_all | solution.py:87
  89.3 129.4 %while.35 = (s32[]{:T(128)}, bf16[4,1,2048,64]{2,3,0,1:T(8,128)(2,1)S(1)}, pred[1,1,1,1]{3,2,1,0:T(4,128)(4,1)}, bf16[4,1,2048,64]{2,3,0,1:T(8,128)(2,1)}, bf16[...) while((s32[]{:T(128)}, ...), condition=%wide.region_5.6_spmd, body=%wide.region_2.5_spmd.sunk | while | flops 275810560 | bytes 11147424 | solution.py:41
  231.0 424.9 %while.36 = (s32[]{:T(128)}, bf16[4,1,2048,64]{2,3,0,1:T(8,128)(2,1)}, f32[4,1,2048,64]{2,3,0,1:T(8,128)}, f32[4,1,2048,64]{2,3,0,1:T(8,128)}, pred[1,1,1,1]{3,2...) while((s32[]{:T(128)}, ...), condition=%wide.region_10.11_spmd.clone, body=%wide.region_6.10_spmd.clone.sunk | while | flops 700488960 | bytes 48052436 | solution.py:65
  244.5 7.7 fusion.176
  269.8 8.3 fusion.176
  296.5 8.3 fusion.176
  323.1 8.3 fusion.176
  349.7 8.3 fusion.176
  376.4 8.3 fusion.176
  403.0 8.3 fusion.176
  429.7 8.3 fusion.176
  456.3 8.3 fusion.176
  482.9 8.3 fusion.176
  509.6 8.3 fusion.176
  536.2 8.3 fusion.176
  562.9 8.3 fusion.176
  589.5 8.3 fusion.176
  616.1 8.3 fusion.176
  642.8 8.3 fusion.176
  667.3 9.0 fusion.132
  676.3 12.7 %reshape.407 = bf16[16,2,49152]{2,1,0:T(2,128)(2,1)} reshape(bf16[2048,3,1,4,64]{4,3,2,1,0:T(4,128)(2,1)} %fusion.132) | data formatting | bytes 6291456
  703.5 29.4 %all-to-all-done.3 = bf16[16,2,49152]{2,1,0:T(2,128)(2,1)} async-done(((bf16[16,2,49152]{2,1,0:T(2,128)(2,1)}), bf16[16,2,49152]{2,1,0:T(2,128)(2,1)}, u32[]{:S(2)}, u32[]{:S(2)}) %all-to-all-start.3) | async-done | bytes 3145760 | tf_op jit(solution)/shard_map/all_to_all | solution.py:96
  733.0 12.3 %reshape.408 = bf16[2048,3,1,4,64]{4,3,2,1,0:T(4,128)(2,1)} reshape(bf16[16,2,49152]{2,1,0:T(2,128)(2,1)} %all-to-all-done.3) | data formatting | bytes 6291456
  745.3 9.9 %copy.116 = bf16[3,4,16,128,64]{3,4,2,0,1:T(8,128)(2,1)} copy(bf16[3,4,16,128,64]{4,1,0,3,2:T(4,128)(2,1)} %bitcast.195) | data formatting | bytes 6291456 | tf_op jit(solution)/shard_map/bsi,tbnsd->itnd/dot_general | solution.py:97
  755.3 8.8 convolution_bitcast_fusion.2
  771.2 7.8 copy.113
  779.0 10.1 %copy.102 = bf16[3,4,1,2048,64]{3,4,2,1,0:T(8,128)(2,1)} copy(bf16[3,4,1,2048,64]{4,1,2,0,3:T(4,128)(2,1)} %bitcast.197) | data formatting | bytes 6291456 | tf_op jit(solution)/shard_map/all_to_all | solution.py:96
  792.7 8.0 convert_reduce_fusion.1
  804.0 34.8 %all-reduce = (f32[1024]{0:T(1024)}, f32[1024]{0:T(1024)}, f32[3072]{0:T(1024)}, f32[1024]{0:T(1024)}) all-reduce(f32[1024]{0:T(1024)S(1)} %get-tuple-element.424, f32[1024]{0:T(1024)S(1)} %get-tuple-element.426, f32[3072]{0:T(1024)S(1)} %reshape.389, f32[1024]{0:T(1024)S(1)} %get-tuple-element.475), channel_id=1, replica_groups=mesh['sp'=16] {'sp'}, use_global_device_ids=true, to_apply=%region_14.15 | all-reduce | flops 6144 | bytes 49152 | tf_op jit(solution)/shard_map/psum | solution.py:104
  838.8 108.8 %all-reduce.4.cloned.1.call-done = (f32[1024,3072]{1,0:T(8,128)}, f32[1024,1024]{1,0:T(8,128)}) async-done(((f32[1024,3072]{1,0:T(8,128)}, f32[1024,1024]{1,0:T(8,128)}), (f32[1024,3072]{1,0:T(8,128)}, f32[1024,1024]{1,0:T(8,128)})) %all-reduce.4.cloned.1.call-update) | async-done | bytes 16777232 | tf_op jit(solution)/shard_map/psum | solution.py:104
  947.6 11.1 %copy.155 = f32[1024,3072]{1,0:T(8,128)} copy(f32[1024,3072]{1,0:T(8,128)} %get-tuple-element.659) | data formatting | bytes 25165824
  (261 shorter events, 514.5 us)
Async XLA Ops:
  11.3 5.3 copy-start
  11.3 6.6 copy-start.19
  11.3 6.6 copy-start.20
  11.3 6.6 copy-start.16
  11.3 24.2 %all-to-all-start.2 = ((bf16[4,16,128,64]{2,3,0,1:T(8,128)(2,1)}), bf16[4,16,128,64]{2,3,0,1:T(8,128)(2,1)S(1)}, u32[]{:S(2)}, u32[]{:S(2)}) async-start(bf16[4,16,128,64]{2,3,0,1:T(8,128)(2,1)} %fusion.112), calls=%async_computation.2 | async-start | bytes 2097152 | tf_op jit(solution)/shard_map/all_to_all | solution.py:93
  16.8 9.9 %copy-start.10 = (f32[4,128]{1,0:T(4,128)}, f32[4,128]{1,0:T(4,128)S(1)}, u32[]{:S(2)}) copy-start(f32[4,128]{1,0:T(4,128)S(1)} %broadcast_multiply_fusion) | copy-start | bytes 6148
  17.3 0.6 copy-start.12
  17.8 8.9 copy-start.14
  17.9 8.8 copy-start.8
  17.9 8.8 copy-start.17
  35.5 5.1 copy-start.22
  35.5 1.0 copy-start.4
  36.5 44.2 %all-to-all-start = ((bf16[3,4,16,128,64]{3,4,0,1,2:T(8,128)(2,1)}), bf16[3,4,16,128,64]{3,4,0,1,2:T(8,128)(2,1)S(1)}, u32[]{:S(2)}, u32[]{:S(2)}) async-start(bf16[3,4,16,128,64]{3,4,0,1,2:T(8,128)(2,1)} %copy.87), calls=%async_computation | async-start | bytes 6291456 | tf_op jit(solution)/shard_map/all_to_all | solution.py:87
  83.9 3.3 copy-start.5
  87.9 1.4 copy-start.6
  218.7 1.0 copy-start.2
  224.8 464.2 %all-to-all-start.1 = ((bf16[16,2,16384]{2,1,0:T(2,128)(2,1)}), bf16[16,2,16384]{2,1,0:T(2,128)(2,1)}, u32[]{:S(2)}, u32[]{:S(2)}) async-start(bf16[16,2,16384]{2,1,0:T(2,128)(2,1)} %reshape.405), calls=%async_computation.1 | async-start | bytes 2097152 | tf_op jit(solution)/shard_map/all_to_all | solution.py:89
  689.0 44.0 %all-to-all-start.3 = ((bf16[16,2,49152]{2,1,0:T(2,128)(2,1)}), bf16[16,2,49152]{2,1,0:T(2,128)(2,1)}, u32[]{:S(2)}, u32[]{:S(2)}) async-start(bf16[16,2,49152]{2,1,0:T(2,128)(2,1)} %reshape.407), calls=%async_computation.3 | async-start | bytes 6291456 | tf_op jit(solution)/shard_map/all_to_all | solution.py:96
  693.0 254.6 %all-reduce.4.cloned.1.call-start = ((), (), s32[]{:S(2)}) async-start(), calls=%async_computation.4 | async-start | bytes 33554432 | tf_op jit(solution)/shard_map/psum | solution.py:104
  745.3 9.9 %copy-start.1 = (bf16[4,128,1024]{2,1,0:T(8,128)(2,1)S(1)}, bf16[4,128,1024]{2,1,0:T(8,128)(2,1)}, u32[]{:S(2)}) copy-start(bf16[4,128,1024]{2,1,0:T(8,128)(2,1)} %param.13) | copy-start | bytes 3145732
  745.3 9.9 %copy-start.9 = (f32[1024]{0:T(1024)S(1)}, f32[1024]{0:T(1024)}, u32[]{:S(2)}) copy-start(f32[1024]{0:T(1024)} %copy-done.8) | copy-start | bytes 12292
  745.3 9.9 %copy-start.11 = (f32[4,128]{1,0:T(4,128)S(1)}, f32[4,128]{1,0:T(4,128)}, u32[]{:S(2)}) copy-start(f32[4,128]{1,0:T(4,128)} %copy-done.10) | copy-start | bytes 6148
  745.3 9.9 %copy-start.15 = (f32[4,128]{1,0:T(4,128)S(1)}, f32[4,128]{1,0:T(4,128)}, u32[]{:S(2)}) copy-start(f32[4,128]{1,0:T(4,128)} %copy-done.14) | copy-start | bytes 6148
  745.3 9.9 %copy-start.18 = (f32[1024]{0:T(1024)S(1)}, f32[1024]{0:T(1024)}, u32[]{:S(2)}) copy-start(f32[1024]{0:T(1024)} %copy-done.17) | copy-start | bytes 12292
  764.1 0.7 copy-start.21
  792.7 8.1 copy-start.13
  800.8 1.3 copy-start.7
  947.6 11.1 %copy-start.3 = (f32[1024,1024]{1,0:T(8,128)S(1)}, f32[1024,1024]{1,0:T(8,128)}, u32[]{:S(2)}) copy-start(f32[1024,1024]{1,0:T(8,128)} %get-tuple-element.661) | copy-start | bytes 12582916
Sparse Core Ops, SparseCore 0:
  764.2 183.2 all-reduce.3
where the time goes:
time: 977 us; the launch traced here: 968 us
  matrix products  572 us (59%)
  waiting for transfers between devices  172 us (18%)
  local copies, waits for them, and re-layouts  117 us (12%)
  other arithmetic  36.4 us (4%)
  blocking collectives  34.8 us (4%)
  starting transfers between devices  18.7 us (2%)
  between operations  15.3 us (2%)
    sub x32, matrix products, score_probs(): return jax.nn.softmax(jnp.where(allowed, logits, NEG_BIG), axis=-1)  147 us
    dot_general x16, matrix products, q_step(): jnp.einsum('bhqk,bhqd->bhkd', d_logit, q_part, preferred_element_type=jnp...  132 us
    psum x1, waiting for transfers between devices, local_block(): lax.psum((d_gamma, d_beta, d_wqkv, d_bqkv, d_wout, d_bout), 'sp')  109 us
    dot_general x16, matrix products, q_step(): jnp.einsum('bhqk,bhkd->bhqd', d_logit, k_all, preferred_element_type=jnp....  105 us
    dot_general x16, matrix products, q_step(): jnp.einsum('bhqk,bhqd->bhkd', prob_bf, do_part, preferred_element_type=jn...  76.8 us
    unnamed x56, local copies, waits for them, and re-layouts  61 us
    dot_general x16, matrix products, q_step(): jnp.einsum('bhqk,bhkd->bhqd', attn_prob.astype(jnp.bfloat16), v_all, pref...  49.9 us
    psum x1, blocking collectives, local_block(): lax.psum((d_gamma, d_beta, d_wqkv, d_bqkv, d_wout, d_bout), 'sp')  34.8 us
  transfers between devices with their start and end apart: 5, of which 3 were waited for; matrix products, arithmetic and copies ran while one was open for 55% of the time, Pallas kernels for 0%

commit v1 on v0

v1 whole, which is shorter than its diff:
```python
import functools
import math

import jax
import jax.numpy as jnp
from jax import lax
from jax.experimental import pallas as pl
from jax.experimental.pallas import tpu as pltpu
from jax.sharding import PartitionSpec as P

LN_EPS = 1e-5
NEG_BIG = -1e30
BF = jnp.bfloat16
F32 = jnp.float32
QB = 256
L = 128
W3 = 384
T = 512
D = 1024
DR = 1032
S = 2048
D3 = 3072
VMEM_CAP = 60 * D * D


def dot_nn(a, b):
    return lax.dot_general(a, b, (((1,), (0,)), ((), ())), preferred_element_type=F32)


def dot_nt(a, b):
    return lax.dot_general(a, b, (((1,), (1,)), ((), ())), preferred_element_type=F32)


def dot_tn(a, b):
    return lax.dot_general(a, b, (((0,), (0,)), ((), ())), preferred_element_type=F32)


def swap_halves(a):
    return jnp.concatenate([a[:, 64:], a[:, :64]], axis=1)


def pair_halves(a, a_half, b, b_half):
    lane = lax.broadcasted_iota(jnp.int32, a.shape, 1)
    a = jnp.where(a_half == 1, swap_halves(a), a)
    b = jnp.where(b_half == 0, swap_halves(b), b)
    return jnp.where(lane < 64, a, b)


def pre_kernel(perm_ref, x_ref, dy_ref, gamma_ref, beta_ref, wout_ref, h_ref, do_ref, wp_ref):
    for c in range(8):
        wp_ref[c * L:c * L + 64] = wout_ref[perm_ref[c]]
        wp_ref[c * L + 64:c * L + L] = wout_ref[perm_ref[8 + c]]
    gamma = gamma_ref[...].astype(F32)
    beta = beta_ref[...].astype(F32)
    for b in range(4):
        xf = x_ref[b].astype(F32)
        cen = xf - jnp.mean(xf, axis=-1, keepdims=True)
        var = jnp.mean(cen * cen, axis=-1, keepdims=True)
        h_ref[b] = (cen * lax.rsqrt(var + LN_EPS) * gamma + beta).astype(BF)
    dy = dy_ref[...].reshape(T, D)
    for c in range(4):
        d = dot_nt(dy, wp_ref[c * QB:(c + 1) * QB]).astype(BF)
        for u in range(2):
            do_ref[2 * c + u] = d[:, u * L:(u + 1) * L].reshape(4, L, L)


def pre_call(perm, x, dy, gamma, beta, wout):
    vm = pl.BlockSpec(memory_space=pltpu.VMEM)
    return pl.pallas_call(
        pre_kernel,
        out_shape=(jax.ShapeDtypeStruct((4, L, D), BF), jax.ShapeDtypeStruct((8, 4, L, L), BF)),
        in_specs=[pl.BlockSpec(memory_space=pltpu.SMEM)] + [vm] * 5,
        out_specs=(vm, vm),
        scratch_shapes=[pltpu.VMEM((D, D), BF)],
        compiler_params=pltpu.CompilerParams(vmem_limit_bytes=VMEM_CAP),
        cost_estimate=pl.CostEstimate(flops=2 * T * D * D, bytes_accessed=8 << 20, transcendentals=0),
        name="pre",
    )(perm, x, dy, gamma, beta, wout)


def attn_kernel(sel_ref, hg_ref, dog_ref, *refs):
    w_refs, bias_refs = refs[:6], refs[6:12]
    send_ref, dwp_ref = refs[12:14]
    w_ref, bias_ref, qkv_ref, dqkv_ref, qt_ref, dot_ref, dkt_ref, dvt_ref = refs[14:22]
    scr = (refs[22:25], refs[25:28])
    b = pl.program_id(0)
    f_half, g_half = sel_ref[1], sel_ref[3]

    @pl.when(b == 0)
    def _():
        for t in range(3):
            w_ref[:, t * L:(t + 1) * L] = pair_halves(w_refs[2 * t][...], f_half, w_refs[2 * t + 1][...], g_half)
            bf = bias_refs[2 * t][0].astype(F32)
            bg = bias_refs[2 * t + 1][0].astype(F32)
            bias_ref[:, t * L:(t + 1) * L] = pair_halves(bf, f_half, bg, g_half)
        dwp_ref[...] = jnp.zeros_like(dwp_ref)

    def qkv_step(r, carry):
        rows = hg_ref[pl.ds(2 * r, 2), 0].reshape(T, D)
        out = dot_nn(rows, w_ref[...]) + bias_ref[0:1, :]
        qkv_ref[pl.ds(pl.multiple_of(r * T, T), T), :] = out.astype(BF)
        return carry

    lax.fori_loop(0, 4, qkv_step, 0)
    for i in range(8):
        qs = qkv_ref[i * QB:(i + 1) * QB, 0:L] * BF(0.125)
        qt_ref[:, i * QB:(i + 1) * QB] = qs.T
        do = dog_ref[2 * i:2 * i + 2, 0].reshape(QB, L)
        dot_ref[:, i * QB:(i + 1) * QB] = do.T
    dkt_ref[...] = jnp.zeros_like(dkt_ref)
    dvt_ref[...] = jnp.zeros_like(dvt_ref)
    lane = lax.broadcasted_iota(jnp.int32, (QB, L), 1)
    row_i = lax.broadcasted_iota(jnp.int32, (QB, QB), 0)
    col_i = lax.broadcasted_iota(jnp.int32, (QB, QB), 1)

    def head_block(i, hd):
        s_ref, p_ref, ds_ref = scr[hd]
        first = 0 if hd == 0 else max(0, i - 2)
        blocks = range(first, i + 1)
        mine = (lane < 64) if hd == 0 else (lane >= 64)
        qi = qkv_ref[i * QB:(i + 1) * QB, 0:L] * BF(0.125)
        doi = dog_ref[2 * i:2 * i + 2, 0].reshape(QB, L)
        qm = jnp.where(mine, qi, BF(0))
        dom = jnp.where(mine, doi, BF(0))
        mx = None
        for kb in blocks:
            s = dot_nt(qm, qkv_ref[kb * QB:(kb + 1) * QB, L:QB])
            if kb == i:
                s = jnp.where(col_i <= row_i, s, NEG_BIG)
            if hd == 1 and kb == i - 2:
                s = jnp.where(col_i > row_i, s, NEG_BIG)
            s_ref[:, (kb - first) * QB:(kb - first + 1) * QB] = s
            cur = jnp.maximum(s[:, :L], s[:, L:])
            mx = cur if mx is None else jnp.maximum(mx, cur)
        m = jnp.max(mx, axis=1, keepdims=True)
        ls = None
        for kb in blocks:
            o_ = (kb - first) * QB
            e = jnp.exp(s_ref[:, o_:o_ + QB] - m)
            s_ref[:, o_:o_ + QB] = e
            cur = e[:, :L] + e[:, L:]
            ls = cur if ls is None else ls + cur
        rl = 1.0 / jnp.sum(ls, axis=1, keepdims=True)
        acc = None
        for kb in blocks:
            o_ = (kb - first) * QB
            p_ = s_ref[:, o_:o_ + QB] * rl
            s_ref[:, o_:o_ + QB] = p_
            pb = p_.astype(BF)
            p_ref[:, o_:o_ + QB] = pb
            cur = dot_nn(pb, qkv_ref[kb * QB:(kb + 1) * QB, QB:W3])
            acc = cur if acc is None else acc + cur
        dsum = jnp.sum(dom.astype(F32) * acc, axis=1, keepdims=True)
        dq = None
        for kb in blocks:
            o_ = (kb - first) * QB
            dp = dot_nt(dom, qkv_ref[kb * QB:(kb + 1) * QB, QB:W3]).astype(BF).astype(F32)
            ds = (s_ref[:, o_:o_ + QB] * (dp - dsum)).astype(BF)
            ds_ref[:, o_:o_ + QB] = ds
            cur = dot_nn(ds, qkv_ref[kb * QB:(kb + 1) * QB, L:QB])
            dq = cur if dq is None else dq + cur
        hr = slice(hd * 64, hd * 64 + 64)
        n = len(blocks) * QB
        dotb = dot_ref[hr, i * QB:(i + 1) * QB]
        qtb = qt_ref[hr, i * QB:(i + 1) * QB]
        dvt_ref[hr, first * QB:first * QB + n] += dot_nn(dotb, p_ref[:, :n])
        dkt_ref[hr, first * QB:first * QB + n] += dot_nn(qtb, ds_ref[:, :n])
        return acc, dq * 0.125

    for i in range(8):
        of, dqf = head_block(i, 0)
        og, dqg = head_block(i, 1)
        o = jnp.where(lane < 64, of, og).astype(BF)
        dq = jnp.where(lane < 64, dqf, dqg).astype(BF)
        for u in range(2):
            send_ref[2 * i + u, 0, 0] = o[u * L:(u + 1) * L]
            send_ref[2 * i + u, 0, 1] = dq[u * L:(u + 1) * L]
        dqkv_ref[i * QB:(i + 1) * QB, 0:L] = dq

    for t, src in ((1, dkt_ref), (2, dvt_ref)):
        for j in range(16):
            d = src[:, j * L:(j + 1) * L].T.astype(BF)
            send_ref[j, 0, 1 + t] = d
            dqkv_ref[j * L:(j + 1) * L, t * L:(t + 1) * L] = d

    def dw_step(r, carry):
        cols = pl.ds(pl.multiple_of(r * QB, QB), QB)
        hc = hg_ref[:, 0, :, cols].reshape(S, QB)
        dwp_ref[cols, :] += dot_tn(hc, dqkv_ref[...])
        return carry

    lax.fori_loop(0, 4, dw_step, 0)
    dwp_ref[D:1025, :] += jnp.sum(dqkv_ref[...].astype(F32), axis=0, keepdims=True)


def attn_call(sel, hg, dog, w_qkv, b_qkv3):
    full = lambda b, s: (0, b, 0, 0)
    in_specs = [pl.BlockSpec((8, 1, QB, D), full), pl.BlockSpec((16, 1, L, L), full)]
    for t in range(3):
        for u in range(2):
            in_specs.append(pl.BlockSpec((D, L), lambda b, s, t=t, u=u: (0, t * 8 + s[2 * u])))
    for t in range(3):
        for u in range(2):
            in_specs.append(pl.BlockSpec((1, 8, L), lambda b, s, t=t, u=u: (t * 8 + s[2 * u], 0, 0)))
    flash = [pltpu.VMEM((QB, S), F32), pltpu.VMEM((QB, S), BF), pltpu.VMEM((QB, S), BF)]
    band = [pltpu.VMEM((QB, 768), F32), pltpu.VMEM((QB, 768), BF), pltpu.VMEM((QB, 768), BF)]
    return pl.pallas_call(
        attn_kernel,
        grid_spec=pltpu.PrefetchScalarGridSpec(
            num_scalar_prefetch=1,
            grid=(2,),
            in_specs=in_specs,
            out_specs=[
                pl.BlockSpec((16, 1, 4, L, L), lambda b, s: (0, b, 0, 0, 0)),
                pl.BlockSpec((DR, W3), lambda b, s: (0, 0)),
            ],
            scratch_shapes=[
                pltpu.VMEM((D, W3), BF), pltpu.VMEM((8, W3), F32),
                pltpu.VMEM((S, W3), BF), pltpu.VMEM((S, W3), BF),
                pltpu.VMEM((L, S), BF), pltpu.VMEM((L, S), BF),
                pltpu.VMEM((L, S), F32), pltpu.VMEM((L, S), F32),
            ] + flash + band,
        ),
        out_shape=[jax.ShapeDtypeStruct((16, 2, 4, L, L), BF), jax.ShapeDtypeStruct((DR, W3), F32)],
        compiler_params=pltpu.CompilerParams(vmem_limit_bytes=VMEM_CAP, dimension_semantics=("arbitrary",)),
        cost_estimate=pl.CostEstimate(flops=40 * 10**9, bytes_accessed=20 << 20, transcendentals=0),
        name="attn",
    )(sel, hg, dog, *([w_qkv] * 6), *([b_qkv3] * 6))


def gather_heads(recv_ref, pos_ref, arr, b, m):
    pa, pb = pos_ref[2 * m], pos_ref[2 * m + 1]
    k, j = b // 2, b % 2
    a = recv_ref[2 * (pa % 8) + k, j, arr]
    c = recv_ref[2 * (pb % 8) + k, j, arr]
    return pair_halves(a, pa // 8, c, pb // 8)


def post_kernel(pos_ref, recv_ref, x_ref, dy_ref, gamma_ref, bout_ref, wqkv_ref, wout_ref,
                y_ref, dx_ref, dwout_ref, small_ref, o_ref, dqkv_ref):
    for b in range(4):
        for m in range(8):
            o_ref[b * L:(b + 1) * L, m * L:(m + 1) * L] = gather_heads(recv_ref, pos_ref, 0, b, m)
            for t in range(3):
                dqkv_ref[b * L:(b + 1) * L, t * D + m * L:t * D + (m + 1) * L] = gather_heads(
                    recv_ref, pos_ref, 1 + t, b, m)
    gamma = gamma_ref[...].astype(F32)
    bout = bout_ref[...].astype(F32)
    dy_all = dy_ref[...].reshape(T, D)
    for c in range(4):
        dwout_ref[c * QB:(c + 1) * QB] = dot_tn(o_ref[:, c * QB:(c + 1) * QB], dy_all)
    dg = jnp.zeros((1, D), F32)
    db = jnp.zeros((1, D), F32)
    dbo = jnp.zeros((1, D), F32)
    for b in range(4):
        rows = slice(b * L, (b + 1) * L)
        xf = x_ref[b].astype(F32)
        dyf = dy_ref[b].astype(F32)
        y_ref[b] = (xf + dot_nn(o_ref[rows], wout_ref[...]) + bout).astype(BF)
        cen = xf - jnp.mean(xf, axis=-1, keepdims=True)
        rstd = lax.rsqrt(jnp.mean(cen * cen, axis=-1, keepdims=True) + LN_EPS)
        xhat = cen * rstd
        dh = dot_nt(dqkv_ref[rows], wqkv_ref[...]).astype(BF).astype(F32)
        dg += jnp.sum(dh * xhat, axis=0, keepdims=True)
        db += jnp.sum(dh, axis=0, keepdims=True)
        dbo += jnp.sum(dyf, axis=0, keepdims=True)
        dxh = dh * gamma
        m1 = jnp.mean(dxh, axis=-1, keepdims=True)
        m2 = jnp.mean(dxh * xhat, axis=-1, keepdims=True)
        dx_ref[b] = (dyf + rstd * (dxh - m1 - xhat * m2)).astype(BF)
    small_ref[...] = jnp.zeros_like(small_ref)
    small_ref[0:1] = dg
    small_ref[1:2] = db
    small_ref[2:3] = dbo


def post_call(pos, recv, x, dy, gamma, bout, wqkv, wout):
    vm = pl.BlockSpec(memory_space=pltpu.VMEM)
    tok = jax.ShapeDtypeStruct((4, L, D), BF)
    return pl.pallas_call(
        post_kernel,
        out_shape=(tok, tok, jax.ShapeDtypeStruct((D, D), F32), jax.ShapeDtypeStruct((8, D), F32)),
        in_specs=[pl.BlockSpec(memory_space=pltpu.SMEM)] + [vm] * 7,
        out_specs=(vm,) * 4,
        scratch_shapes=[pltpu.VMEM((T, D), BF), pltpu.VMEM((T, D3), BF)],
        compiler_params=pltpu.CompilerParams(vmem_limit_bytes=VMEM_CAP),
        cost_estimate=pl.CostEstimate(flops=10 * 10**9, bytes_accessed=24 << 20, transcendentals=0),
        name="post",
    )(pos, recv, x, dy, gamma, bout, wqkv, wout)


def unpack_kernel(pos_ref, dw_ref, out_ref):
    r = pl.program_id(1)
    m = r % 8
    pa, pb = pos_ref[2 * m], pos_ref[2 * m + 1]
    a = dw_ref[pa % 8]
    c = dw_ref[pb % 8]
    out_ref[...] = pair_halves(a, pa // 8, c, pb // 8)


def unpack_call(pos, dwg):
    return pl.pallas_call(
        unpack_kernel,
        grid_spec=pltpu.PrefetchScalarGridSpec(
            num_scalar_prefetch=1,
            grid=(3, 8),
            in_specs=[pl.BlockSpec((8, DR, L), lambda t, m, s: (0, 0, t))],
            out_specs=pl.BlockSpec((DR, L), lambda t, m, s: (0, t * 8 + m)),
        ),
        out_shape=jax.ShapeDtypeStruct((DR, D3), F32),
        compiler_params=pltpu.CompilerParams(vmem_limit_bytes=VMEM_CAP),
        name="unpack",
    )(pos, dwg)


def solution(mesh):
    tok_spec = P(None, "sp", None)

    def local_block(x, d_y, ln_gamma, ln_beta, w_qkv, b_qkv, w_out, b_out, head_kind):
        me = lax.axis_index("sp")
        chip, core = me // 2, me % 2
        idx = jnp.arange(16, dtype=jnp.int32)
        same_before = (head_kind[None, :] == head_kind[:, None]) & (idx[None, :] < idx[:, None])
        pos = jnp.sum(same_before.astype(jnp.int32), axis=1) + 8 * head_kind
        perm = jnp.sum(jnp.where(pos[None, :] == idx[:, None], idx[None, :], 0), axis=1)
        f, g = perm[chip], perm[8 + chip]
        sel = jnp.stack([f // 2, f % 2, g // 2, g % 2])
        gamma2, beta2, bout2 = (v.reshape(1, D) for v in (ln_gamma, ln_beta, b_out))
        h, do = pre_call(perm, x, d_y, gamma2, beta2, w_out.reshape(16, 64, D))
        h2 = h.reshape(2, 2, L, D)
        mine = jnp.where(core == 0, h2[0], h2[1])
        other = jnp.where(core == 0, h2[1], h2[0])
        got = lax.ppermute(other, "sp", [(d, d ^ 1) for d in range(16)])
        blk = jnp.stack([jnp.where(core == 0, mine, got), jnp.where(core == 0, got, mine)], axis=1)
        blk = blk.reshape(2, QB, D)
        hg = lax.all_gather(blk, "sp", axis_index_groups=[list(range(0, 16, 2)), list(range(1, 16, 2))])
        dog = lax.all_to_all(do.reshape(16, 2, L, L), "sp", 0, 0, tiled=True)
        b3 = jnp.broadcast_to(b_qkv.reshape(24, 1, L), (24, 8, L))
        send, dwp = attn_call(sel, hg, dog, w_qkv, b3)
        recv = lax.all_to_all(send, "sp", 0, 0, tiled=True)
        y, dx, dwout, small = post_call(pos, recv, x, d_y, gamma2, bout2, w_qkv, w_out)
        dwg = lax.all_gather(dwp, "sp").reshape(8, 2, DR, W3)
        dw = unpack_call(pos, dwg[:, 0] + dwg[:, 1])
        dwout, small = lax.psum((dwout, small), "sp")
        return y, dx, small[0], small[1], dw[:D], dw[D], dwout, small[2]

    return jax.shard_map(
        local_block, mesh=mesh,
        in_specs=(tok_spec, tok_spec, P(), P(), P(), P(), P(), P(), P()),
        out_specs=(tok_spec, tok_spec, P(), P(), P(), P(), P(), P()), check_vma=False)
```

time: 977 us -> 406 us (0.42)
  matrix products: 572 us -> 0 us
  Pallas kernels: 0 us -> 103 us
  local copies, waits for them, and re-layouts: 117 us -> 23.3 us
  waiting for transfers between devices: 172 us -> 196 us
  other arithmetic: 36.4 us -> 19.5 us
    dot_general x86 -> x0, matrix products: 425 us -> none  [the longest x16 132 us: q_step(): jnp.einsum('bhqk,bhqd->bhkd', d_logit, q_part, preferred_element_type=jnp...]
    sub x32 -> x0, matrix products: 147 us -> none  [score_probs(): return jax.nn.softmax(jnp.where(allowed, logits, NEG_BIG), axis=-1)]
    pallas_call x0 -> x4, Pallas kernels: none -> 103 us  [the longest x1 56 us: attn_call(): pl.pallas_call(attn_kernel, grid_spec=pltpu.PrefetchScalarGridSpec(num_sc...]
    all_gather x0 -> x2, waiting for transfers between devices: none -> 78.3 us  [the longest x1 55.1 us: local_block(): lax.all_gather(blk, 'sp', axis_index_groups=[list(range(0, 16, 2)), list(...]
    psum x1, waiting for transfers between devices: 109 us -> 36.2 us  [local_block(): dwout, small = lax.psum((dwout, small), 'sp')]
    unnamed x56 -> x11, local copies, waits for them, and re-layouts: 61 us -> 4.81 us
    all_to_all x5 -> x0, local copies, waits for them, and re-layouts: 25.1 us -> none  [the longest x2 17.9 us: local_block(): d_qkv_tok = lax.all_to_all(d_qkv_head, 'sp', 3, 2, tiled=True)]
    and x32 -> x0, other arithmetic: 16.9 us -> none  [score_probs(): (key_pos <= query_pos) & (jnp.logical_not(is_banded) | (key_pos > query_p...]
  transfers between devices with their start and end apart: 5 -> 6, of which waited for: 3 -> 6; matrix products, arithmetic and copies ran while one was open for 55% -> 7% of each run, Pallas kernels for 0% -> 10%
where the time goes in v1:
time: 406 us; the launch traced here: 405 us
  waiting for transfers between devices  196 us (48%)
  Pallas kernels  103 us (25%)
  blocking collectives  34.7 us (9%)
  local copies, waits for them, and re-layouts  23.3 us (6%)
  other arithmetic  19.5 us (5%)
  between operations  19.1 us (5%)
  starting transfers between devices  9.37 us (2%)
    all_to_all x1, waiting for transfers between devices, local_block(): recv = lax.all_to_all(send, 'sp', 0, 0, tiled=True)  62.6 us
    pallas_call x1, Pallas kernels, attn_call(): pl.pallas_call(attn_kernel, grid_spec=pltpu.PrefetchScalarGridSpec(num_sc...  56 us
    all_gather x1, waiting for transfers between devices, local_block(): lax.all_gather(blk, 'sp', axis_index_groups=[list(range(0, 16, 2)), list(...  55.1 us
    psum x1, waiting for transfers between devices, local_block(): dwout, small = lax.psum((dwout, small), 'sp')  36.2 us
    psum x1, blocking collectives, local_block(): dwout, small = lax.psum((dwout, small), 'sp')  34.7 us
    all_gather x1, waiting for transfers between devices, local_block(): dwg = lax.all_gather(dwp, 'sp').reshape(8, 2, DR, W3)  23.1 us
    pallas_call x1, Pallas kernels, unpack_call(): pl.pallas_call(unpack_kernel, grid_spec=pltpu.PrefetchScalarGridSpec(num_...  21.3 us
    pallas_call x1, Pallas kernels, post_call(): pl.pallas_call(post_kernel, out_shape=(tok, tok, jax.ShapeDtypeStruct((D,...  20.5 us
  transfers between devices with their start and end apart: 6, of which 6 were waited for; matrix products, arithmetic and copies ran while one was open for 7% of the time, Pallas kernels for 10%

profile of v1, /device:TPU:0, one launch (start us, length us, event | category | flops | bytes accessed | tf_op | source)
XLA Modules:
  0.0 404.6 jit_solution(6623258670116708742)
XLA Ops:
  7.2 0.9 convert_reduce_fusion
  8.1 0.7 multiply_add_fusion.pos_ref
  8.8 0.6 select_reduce_fusion.perm_ref
  9.4 1.3 reshape.45.gamma_ref
  10.7 1.3 reshape.46.beta_ref
  12.0 5.3 %pre.1 = (bf16[4,128,1024]{2,1,0:T(8,128)(2,1)}, bf16[8,4,128,128]{3,2,1,0:T(8,128)(2,1)}) custom-call(s32[16]{0:T(128)} %select_reduce_fusion.perm_ref, bf16[4,128,1024]{2,1,0:T(8,128)(2,1)} %x_ref.3, bf16[4,128,1024]{2,1,0:T(8,128)(2,1)} %dy_ref.3, bf16[1,1024]{1,0:T(2,128)(2,1)} %reshape.45.gamma_ref, bf16[1,1024]{1,0:T(2,128)(2,1)} %reshape.46.beta_ref, ...), custom_call_target="tpu_custom_call" | custom-call | flops 1073741824 | bytes 8388608 | tf_op jit(solution)/shard_map/pre/pallas_call | solution.py:69
  17.3 1.3 broadcast_select_fusion
  18.5 0.8 collective-permute-start
  19.3 1.5 collective-permute-done
  20.9 1.3 select_bitcast_fusion.1
  22.1 0.1 pad_maximum_fusion
  22.3 1.0 copy.26
  23.3 4.9 %all-to-all-start = ((bf16[16,2,128,128]{3,2,1,0:T(8,128)(2,1)}), bf16[16,2,128,128]{3,2,1,0:T(8,128)(2,1)S(1)}, u32[]{:S(2)}, u32[]{:S(2)}) async-start(bf16[16,2,128,128]{3,2,1,0:T(8,128)(2,1)} %bitcast.10), calls=%async_computation | async-start | bytes 2097152 | tf_op jit(solution)/shard_map/all_to_all | solution.py:337
  28.3 0.6 fusion.4
  34.1 0.7 pad_add_fusion.sel_ref
  34.8 16.9 %all-to-all-done.dog_ref = bf16[16,2,128,128]{3,2,1,0:T(8,128)(2,1)S(1)} async-done(((bf16[16,2,128,128]{3,2,1,0:T(8,128)(2,1)}), bf16[16,2,128,128]{3,2,1,0:T(8,128)(2,1)S(1)}, u32[]{:S(2)}, u32[]{:S(2)}) %all-to-all-start) | async-done | bytes 1048608 | tf_op jit(solution)/shard_map/all_to_all | solution.py:337
  51.8 55.1 %all-gather.4.cloned.1.call-done.hg_ref = bf16[8,2,256,1024]{3,2,1,0:T(8,128)(2,1)} async-done(((bf16[1,2,256,1024]{3,2,1,0:T(8,128)(2,1)}), bf16[8,2,256,1024]{3,2,1,0:T(8,128)(2,1)}) %all-gather.4.cloned.1.call-update) | async-done | bytes 8388624 | tf_op jit(solution)/shard_map/all_gather | solution.py:336
  106.9 0.6 broadcast_in_dim.16.refs_6_.refs_7_.refs_8_.refs_9_.refs_10_.refs_11_
  107.5 56.0 %attn.1 = (bf16[16,2,4,128,128]{4,3,2,1,0:T(8,128)(2,1)}, f32[1032,384]{1,0:T(8,128)}) custom-call(s32[4]{0:T(128)} %pad_add_fusion.sel_ref, bf16[8,2,256,1024]{3,2,1,0:T(8,128)(2,1)} %all-gather.4.cloned.1.call-done.hg_ref, bf16[16,2,128,128]{3,2,1,0:T(8,128)(2,1)} %copy-done, bf16[1024,3072]{1,0:T(8,128)(2,1)} %wqkv_ref.1, bf16[1024,3072]{1,0:T(8,128)(2,1)} %wqkv_ref.1, ...), custom_call_target="tpu_custom_call" | custom-call | flops 40000000000 | bytes 20971520 | tf_op jit(solution)/shard_map/attn/pallas_call | solution.py:207
  163.6 3.5 all-to-all-start.1
  167.2 0.6 reshape.49.bout_ref
  167.8 62.6 %all-to-all-done.1.recv_ref = bf16[16,2,4,128,128]{4,3,2,1,0:T(8,128)(2,1)} async-done(((bf16[16,2,4,128,128]{4,3,2,1,0:T(8,128)(2,1)}), bf16[16,2,4,128,128]{4,3,2,1,0:T(8,128)(2,1)}, u32[]{:S(2)}, u32[]{:S(2)}) %all-to-all-start.1) | async-done | bytes 4194336 | tf_op jit(solution)/shard_map/all_to_all | solution.py:340
  230.4 20.5 %post.1 = (bf16[4,128,1024]{2,1,0:T(8,128)(2,1)}, bf16[4,128,1024]{2,1,0:T(8,128)(2,1)}, f32[1024,1024]{1,0:T(8,128)}, f32[8,1024]{1,0:T(8,128)}) custom-call(s32[16]{0:T(128)} %copy-done.4, bf16[16,2,4,128,128]{4,3,2,1,0:T(8,128)(2,1)} %all-to-all-done.1.recv_ref, bf16[4,128,1024]{2,1,0:T(8,128)(2,1)} %x_ref.3, bf16[4,128,1024]{2,1,0:T(8,128)(2,1)} %dy_ref.3, ...), custom_call_target="tpu_custom_call" | custom-call | flops 10000000000 | bytes 25165824 | tf_op jit(solution)/shard_map/post/pallas_call | solution.py:280
  251.0 34.7 %psum.14 = f32[8,1024]{1,0:T(8,128)S(1)} all-reduce(f32[8,1024]{1,0:T(8,128)} %get-tuple-element.21), channel_id=1, replica_groups=mesh['sp'=16] {'sp'}, use_global_device_ids=true, to_apply=%region_2.3 | all-reduce | flops 8192 | bytes 65536 | tf_op jit(solution)/shard_map/psum | solution.py:344
  285.6 0.6 fusion.3
  286.2 23.1 %all-gather.6.cloned.1.call-done = f32[16512,384]{1,0:T(8,128)} async-done(((f32[1032,384]{1,0:T(8,128)}), f32[16512,384]{1,0:T(8,128)}) %all-gather.6.cloned.1.call-update) | async-done | bytes 25362448 | tf_op jit(solution)/shard_map/all_gather | solution.py:342
  309.4 14.0 %fusion.1.dw_ref = f32[8,1032,384]{2,1,0:T(8,128)} fusion(f32[8,2,1032,384]{3,2,1,0:T(8,128)} %bitcast.31), kind=kLoop, calls=%fused_computation.2 | loop fusion | flops 3170304 | bytes 38043648 | tf_op jit(solution)/shard_map/add | solution.py:343
  323.4 21.3 %unpack.1 = f32[1032,3072]{1,0:T(8,128)} custom-call(s32[16]{0:T(128)} %copy-done.4, f32[8,1032,384]{2,1,0:T(8,128)} %fusion.1.dw_ref), custom_call_target="tpu_custom_call" | custom-call | tf_op jit(solution)/shard_map/unpack/pallas_call | solution.py:302
  344.7 11.0 %slice.44 = f32[1024,3072]{1,0:T(8,128)} slice(f32[1032,3072]{1,0:T(8,128)} %unpack.1), slice={[0:1024], [0:3072]} | slice | bytes 25165824 | tf_op jit(solution)/shard_map/slice | solution.py:345
  355.7 1.5 slice.45
  357.2 36.2 %all-reduce.2.cloned.1.call-done = f32[1024,1024]{1,0:T(8,128)} async-done(((f32[1024,1024]{1,0:T(8,128)}), f32[1024,1024]{1,0:T(8,128)}) %all-reduce.2.cloned.1.call-update) | async-done | bytes 4194320 | tf_op jit(solution)/shard_map/psum | solution.py:344
  393.3 4.8 %copy.32 = f32[1024,1024]{1,0:T(8,128)} copy(f32[1024,1024]{1,0:T(8,128)} %all-reduce.2.cloned.1.call-done) | data formatting | bytes 8388608
  (16 shorter events, 0.2 us)
Async XLA Ops:
  7.2 99.7 %copy-start.1 = (bf16[3072]{0:T(1024)(128)(2,1)S(1)}, bf16[3072]{0:T(1024)(128)(2,1)}, u32[]{:S(2)}) copy-start(bf16[3072]{0:T(1024)(128)(2,1)} %param.14) | copy-start | bytes 18436
  7.2 99.7 %all-gather.4.cloned.1.call-start = ((), (), s32[]{:S(2)}) async-start(), calls=%async_computation.2 | async-start | bytes 9437184 | tf_op jit(solution)/shard_map/all_gather | solution.py:336
  8.8 154.7 %copy-start.4 = (s32[16]{0:T(128)}, s32[16]{0:T(128)S(1)}, u32[]{:S(2)}) copy-start(s32[16]{0:T(128)S(1)} %multiply_add_fusion.pos_ref) | copy-start | bytes 196
  9.4 18.9 %copy-start.2 = (s32[16]{0:T(128)S(1)}, s32[16]{0:T(128)}, u32[]{:S(2)}) copy-start(s32[16]{0:T(128)} %select_reduce_fusion.perm_ref) | copy-start | bytes 196
  18.5 2.3 collective-permute-start
  23.3 28.4 %all-to-all-start = ((bf16[16,2,128,128]{3,2,1,0:T(8,128)(2,1)}), bf16[16,2,128,128]{3,2,1,0:T(8,128)(2,1)S(1)}, u32[]{:S(2)}, u32[]{:S(2)}) async-start(bf16[16,2,128,128]{3,2,1,0:T(8,128)(2,1)} %bitcast.10), calls=%async_computation | async-start | bytes 2097152 | tf_op jit(solution)/shard_map/all_to_all | solution.py:337
  28.3 281.1 %all-gather.6.cloned.1.call-start = ((), (), s32[]{:S(2)}) async-start(), calls=%async_computation.4 | async-start | bytes 26947584 | tf_op jit(solution)/shard_map/all_gather | solution.py:342
  51.7 55.8 %copy-start = (bf16[16,2,128,128]{3,2,1,0:T(8,128)(2,1)}, bf16[16,2,128,128]{3,2,1,0:T(8,128)(2,1)S(1)}, u32[]{:S(2)}) copy-start(bf16[16,2,128,128]{3,2,1,0:T(8,128)(2,1)S(1)} %all-to-all-done.dog_ref) | copy-start | bytes 3145732
  163.5 3.6 copy-start.3
  163.6 66.8 %all-to-all-start.1 = ((bf16[16,2,4,128,128]{4,3,2,1,0:T(8,128)(2,1)}), bf16[16,2,4,128,128]{4,3,2,1,0:T(8,128)(2,1)}, u32[]{:S(2)}, u32[]{:S(2)}) async-start(bf16[16,2,4,128,128]{4,3,2,1,0:T(8,128)(2,1)} %get-tuple-element.18), calls=%async_computation.1 | async-start | bytes 8388608 | tf_op jit(solution)/shard_map/all_to_all | solution.py:340
  167.1 226.2 %all-reduce.2.cloned.1.call-start = ((), (), s32[]{:S(2)}) async-start(), calls=%async_computation.3 | async-start | bytes 8388608 | tf_op jit(solution)/shard_map/psum | solution.py:344
Sparse Core Ops, SparseCore 0:
  23.4 83.3 all-gather.3
  163.7 145.6 all-gather.5
  314.6 78.6 all-reduce.1

commit v2 on v1

v2 whole, which is shorter than its diff:
```python
import functools
import math

import jax
import jax.numpy as jnp
from jax import lax
from jax.experimental import pallas as pl
from jax.experimental.pallas import tpu as pltpu
from jax.sharding import PartitionSpec as P

LN_EPS = 1e-5
NEG_BIG = -1e30
BF = jnp.bfloat16
F32 = jnp.float32
QB = 256
L = 128
W3 = 384
T = 512
D = 1024
DR = 1040
HR = 520
N = 16
R3, R4, R8 = range(3), range(4), range(8)
MESH = pl.DeviceIdType.MESH
H_ROWS = (0, 176, 352, 512)
W_ROWS = (0, 176, 352, 520)
O_ROWS = (0, 24, 48, 64)
S = 2048
D3 = 3072
VMEM_CAP = 60 * D * D


def dot_nn(a, b):
    return lax.dot_general(a, b, (((1,), (0,)), ((), ())), preferred_element_type=F32)


def dot_nt(a, b):
    return lax.dot_general(a, b, (((1,), (1,)), ((), ())), preferred_element_type=F32)


def dot_tn(a, b):
    return lax.dot_general(a, b, (((0,), (0,)), ((), ())), preferred_element_type=F32)


def swap_halves(a):
    return jnp.concatenate([a[:, 64:], a[:, :64]], axis=1)


def pair_halves(a, a_half, b, b_half):
    lane = lax.broadcasted_iota(jnp.int32, a.shape, 1)
    a = jnp.where(a_half == 1, swap_halves(a), a)
    b = jnp.where(b_half == 0, swap_halves(b), b)
    return jnp.where(lane < 64, a, b)


class Place:
    def __init__(self):
        self.me = lax.axis_index("sp")
        self.core, self.chip = self.me % 2, self.me // 2
        self.sib = self.me + 1 - 2 * self.core
        bits = (self.chip % 2, self.chip // 2 % 2, self.chip // 4)
        self.step = [(1 - 2 * v) * w for v, w in zip(bits, (1, 2, 4))]

    def chip_at(self, axes):
        out = self.chip
        for a in axes:
            out = out + self.step[a]
        return out

    def next_dev(self, axis):
        return self.me + 2 * self.step[axis]


def rcopy(src, dst, send, recv, dev):
    return pltpu.make_async_remote_copy(
        src_ref=src, dst_ref=dst, send_sem=send, recv_sem=recv, device_id=(dev,), device_id_type=MESH)


def subsets(axes):
    out = [()]
    for a in axes:
        out += [v + (a,) for v in out]
    return out


class Tree:
    def __init__(self, place, own, slot, send, recv):
        self.place, self.own, self.slot, self.send, self.recv = place, own, slot, send, recv
        self.entries = []
        for s in R3:
            for p in R3:
                order = [(p + j) % 3 for j in R3]
                for sub in subsets(order[:s]):
                    self.entries.append((p, order[s], sub))

    def copy(self, e):
        p, axis, sub = e
        i = self.entries.index(e)
        at = self.slot(self.place.chip_at(sub), p)
        return rcopy(at if sub else self.own(p), at, self.send.at[i], self.recv.at[i], self.place.next_dev(axis))

    def start_own(self):
        for e in self.entries:
            if not e[2]:
                self.copy(e).start()

    def arrive(self, e):
        p, axis, sub = e
        got = sub + (axis,)
        chip = self.place.chip_at(got)
        at = self.slot(chip, p)
        i = self.entries.index(e)
        rcopy(at, at, self.send.at[i], self.recv.at[i], self.place.next_dev(axis)).wait_recv()
        for n in self.entries:
            if n[0] == p and n[2] == got:
                self.copy(n).start()
        return chip, p

    def level(self, s):
        return [e for e in self.entries if len(e[2]) <= s and (e[1] - e[0]) % 3 == s]

    def finish(self):
        for e in self.entries:
            self.copy(e).wait_send()


def barrier_signal(place):
    sem = pltpu.get_barrier_semaphore()
    for r in range(1, N):
        pl.semaphore_signal(sem, inc=1, device_id=((place.me + r) % N,), device_id_type=MESH)


def barrier_wait():
    pl.semaphore_wait(pltpu.get_barrier_semaphore(), N - 1)


def head_places(kind_ref):
    pos, zeros, ones = [], 0, 8
    for n in range(N):
        k = kind_ref[n]
        pos.append(jnp.where(k == 0, zeros, ones))
        zeros, ones = zeros + 1 - k, ones + k
    return pos


def exchange(place, src, dst, send, recv):
    out = []
    for r in range(1, N):
        to = (place.me + r) % N
        cp = rcopy(src(to), dst(place.me), send.at[r], recv.at[r], to)
        cp.start()
        out.append(cp)
    return out


def exchange_wait(place, dst, send, recv):
    for r in range(1, N):
        at = dst((place.me + N - r) % N)
        rcopy(at, at, send.at[r], recv.at[r], place.me).wait_recv()


def pre_kernel(kind_ref, x_ref, dy_ref, gamma_ref, beta_ref, wout_hbm, hg_ref, dog_ref, sel_ref,
               blk_ref, out_ref, wout_ref, wp_ref, do_ref, loc_sem, sib_send, sib_recv, ag_send, ag_recv, do_send, do_recv):
    pc = Place()
    barrier_signal(pc)
    w_in = pltpu.make_async_copy(wout_hbm, wout_ref, loc_sem.at[0])
    w_in.start()
    gamma = gamma_ref[...].reshape(1, D).astype(F32)
    beta = beta_ref[...].reshape(1, D).astype(F32)

    def norm(xb):
        xf = xb.astype(F32)
        cen = xf - jnp.mean(xf, axis=-1, keepdims=True)
        var = jnp.mean(cen * cen, axis=-1, keepdims=True)
        return (cen * lax.rsqrt(var + LN_EPS) * gamma + beta).astype(BF)

    for j in range(2):
        out_ref[j] = norm(x_ref[2 * (1 - pc.core) + j])
    for j in range(2):
        blk_ref[j, pc.core] = norm(x_ref[2 * pc.core + j])
    barrier_wait()
    sib = [rcopy(out_ref.at[j], blk_ref.at[j, pc.core], sib_send.at[j], sib_recv.at[j], pc.sib) for j in range(2)]
    for cp in sib:
        cp.start()
    pos = head_places(kind_ref)
    perm = []
    for j in range(N):
        v = 0
        for n in range(1, N):
            v = v + jnp.where(pos[n] == j, n, 0)
        perm.append(v)
    f = g = 0
    for c in R8:
        f = f + jnp.where(pc.chip == c, perm[c], 0)
        g = g + jnp.where(pc.chip == c, perm[8 + c], 0)
    for i, v in enumerate((f // 2, f % 2, g // 2, g % 2)):
        sel_ref[i] = v
    for j in range(2):
        rcopy(blk_ref.at[j, 1 - pc.core], blk_ref.at[j, 1 - pc.core], sib_send.at[j], sib_recv.at[j], pc.sib).wait_recv()

    def rows(p):
        return pl.ds(H_ROWS[p], H_ROWS[p + 1] - H_ROWS[p])

    flat = blk_ref.reshape(T, D)
    tree = Tree(pc, lambda p: flat.at[rows(p)], lambda c, p: hg_ref.at[c, rows(p)], ag_send, ag_recv)
    tree.start_own()
    local = pltpu.make_async_copy(flat, hg_ref.at[pc.chip], loc_sem.at[1])
    local.start()
    w_in.wait()
    for c in R8:
        wp_ref[c * L:c * L + 64] = wout_ref[perm[c]]
        wp_ref[c * L + 64:c * L + L] = wout_ref[perm[8 + c]]
    dy = dy_ref[...].reshape(T, D)
    for c in R4:
        d = dot_nt(dy, wp_ref[c * QB:(c + 1) * QB]).astype(BF)
        for u in range(2):
            do_ref[2 * c + u] = d[:, u * L:(u + 1) * L].reshape(4, L, L)
    for e in tree.level(0):
        tree.arrive(e)
    mine = do_ref.reshape(N, 2, L, L)
    copies = exchange(pc, lambda t: mine.at[t], lambda t: dog_ref.at[t], do_send, do_recv)
    keep = pltpu.make_async_copy(mine.at[pc.me], dog_ref.at[pc.me], loc_sem.at[2])
    keep.start()
    for s in (1, 2):
        for e in tree.level(s):
            tree.arrive(e)
    exchange_wait(pc, lambda t: dog_ref.at[t], do_send, do_recv)
    local.wait()
    keep.wait()
    tree.finish()
    for cp in copies + sib:
        cp.wait_send()


def pre_call(kind, x, dy, gamma, beta, wout):
    vm, sm, hb = (pl.BlockSpec(memory_space=m) for m in (pltpu.VMEM, pltpu.SMEM, pl.ANY))
    sem = pltpu.SemaphoreType.DMA
    return pl.pallas_call(
        pre_kernel,
        out_shape=(jax.ShapeDtypeStruct((8, T, D), BF), jax.ShapeDtypeStruct((N, 2, L, L), BF),
                   jax.ShapeDtypeStruct((4,), jnp.int32)),
        in_specs=[sm, vm, vm, vm, vm, hb],
        out_specs=(hb, hb, sm),
        scratch_shapes=[
            pltpu.VMEM((2, 2, L, D), BF), pltpu.VMEM((2, L, D), BF), pltpu.VMEM((N, 64, D), BF),
            pltpu.VMEM((D, D), BF), pltpu.VMEM((8, 4, L, L), BF),
            sem((3,)), sem((2,)), sem((2,)), sem((21,)), sem((21,)), sem((N,)), sem((N,))],
        compiler_params=pltpu.CompilerParams(vmem_limit_bytes=VMEM_CAP, collective_id=0, has_side_effects=True),
        name="pre",
    )(kind, x, dy, gamma, beta, wout)


def attn_kernel(sel_ref, hg_ref, dog_ref, *refs):
    w_refs, bias_refs = refs[:6], refs[6:12]
    so_ref, sd_ref, dwp_ref = refs[12:15]
    w_ref, bias_ref, qkv_ref, dqkv_ref, qt_ref, dot_ref, dkt_ref, dvt_ref = refs[15:23]
    scr = (refs[23:26], refs[26:29])
    b = pl.program_id(0)
    f_half, g_half = sel_ref[1], sel_ref[3]

    @pl.when(b == 0)
    def _():
        for t in R3:
            w_ref[:, t * L:(t + 1) * L] = pair_halves(w_refs[2 * t][...], f_half, w_refs[2 * t + 1][...], g_half)
            bf = bias_refs[2 * t][0].astype(F32)
            bg = bias_refs[2 * t + 1][0].astype(F32)
            bias_ref[:, t * L:(t + 1) * L] = pair_halves(bf, f_half, bg, g_half)
        dwp_ref[...] = jnp.zeros_like(dwp_ref)

    def qkv_step(r, carry):
        rows = hg_ref[pl.ds(2 * r, 2), 0].reshape(T, D)
        out = dot_nn(rows, w_ref[...]) + bias_ref[0:1, :]
        qkv_ref[pl.ds(pl.multiple_of(r * T, T), T), :] = out.astype(BF)
        return carry

    lax.fori_loop(0, 4, qkv_step, 0)
    for i in R8:
        qs = qkv_ref[i * QB:(i + 1) * QB, 0:L] * BF(0.125)
        qt_ref[:, i * QB:(i + 1) * QB] = qs.T
        do = dog_ref[2 * i:2 * i + 2, 0].reshape(QB, L)
        dot_ref[:, i * QB:(i + 1) * QB] = do.T
    dkt_ref[...] = jnp.zeros_like(dkt_ref)
    dvt_ref[...] = jnp.zeros_like(dvt_ref)
    lane = lax.broadcasted_iota(jnp.int32, (QB, L), 1)
    row_i = lax.broadcasted_iota(jnp.int32, (QB, QB), 0)
    col_i = lax.broadcasted_iota(jnp.int32, (QB, QB), 1)

    def head_block(i, hd):
        s_ref, p_ref, ds_ref = scr[hd]
        first = 0 if hd == 0 else max(0, i - 2)
        blocks = range(first, i + 1)
        mine = (lane < 64) if hd == 0 else (lane >= 64)
        qi = qkv_ref[i * QB:(i + 1) * QB, 0:L] * BF(0.125)
        doi = dog_ref[2 * i:2 * i + 2, 0].reshape(QB, L)
        qm = jnp.where(mine, qi, BF(0))
        dom = jnp.where(mine, doi, BF(0))
        mx = None
        for kb in blocks:
            s = dot_nt(qm, qkv_ref[kb * QB:(kb + 1) * QB, L:QB])
            if kb == i:
                s = jnp.where(col_i <= row_i, s, NEG_BIG)
            if hd == 1 and kb == i - 2:
                s = jnp.where(col_i > row_i, s, NEG_BIG)
            s_ref[:, (kb - first) * QB:(kb - first + 1) * QB] = s
            cur = jnp.maximum(s[:, :L], s[:, L:])
            mx = cur if mx is None else jnp.maximum(mx, cur)
        m = jnp.max(mx, axis=1, keepdims=True)
        ls = None
        for kb in blocks:
            o_ = (kb - first) * QB
            e = jnp.exp(s_ref[:, o_:o_ + QB] - m)
            s_ref[:, o_:o_ + QB] = e
            cur = e[:, :L] + e[:, L:]
            ls = cur if ls is None else ls + cur
        rl = 1.0 / jnp.sum(ls, axis=1, keepdims=True)
        acc = None
        for kb in blocks:
            o_ = (kb - first) * QB
            p_ = s_ref[:, o_:o_ + QB] * rl
            s_ref[:, o_:o_ + QB] = p_
            pb = p_.astype(BF)
            p_ref[:, o_:o_ + QB] = pb
            cur = dot_nn(pb, qkv_ref[kb * QB:(kb + 1) * QB, QB:W3])
            acc = cur if acc is None else acc + cur
        dsum = jnp.sum(dom.astype(F32) * acc, axis=1, keepdims=True)
        dq = None
        for kb in blocks:
            o_ = (kb - first) * QB
            dp = dot_nt(dom, qkv_ref[kb * QB:(kb + 1) * QB, QB:W3]).astype(BF).astype(F32)
            ds = (s_ref[:, o_:o_ + QB] * (dp - dsum)).astype(BF)
            ds_ref[:, o_:o_ + QB] = ds
            cur = dot_nn(ds, qkv_ref[kb * QB:(kb + 1) * QB, L:QB])
            dq = cur if dq is None else dq + cur
        hr = slice(hd * 64, hd * 64 + 64)
        n = len(blocks) * QB
        dotb = dot_ref[hr, i * QB:(i + 1) * QB]
        qtb = qt_ref[hr, i * QB:(i + 1) * QB]
        dvt_ref[hr, first * QB:first * QB + n] += dot_nn(dotb, p_ref[:, :n])
        dkt_ref[hr, first * QB:first * QB + n] += dot_nn(qtb, ds_ref[:, :n])
        return acc, dq * 0.125

    for i in R8:
        of, dqf = head_block(i, 0)
        og, dqg = head_block(i, 1)
        o = jnp.where(lane < 64, of, og).astype(BF)
        dq = jnp.where(lane < 64, dqf, dqg).astype(BF)
        for u in range(2):
            so_ref[2 * i + u, 0] = o[u * L:(u + 1) * L]
            sd_ref[2 * i + u, 0, 0] = dq[u * L:(u + 1) * L]
        dqkv_ref[i * QB:(i + 1) * QB, 0:L] = dq

    for t, src in ((1, dkt_ref), (2, dvt_ref)):
        for j in range(16):
            d = src[:, j * L:(j + 1) * L].T.astype(BF)
            sd_ref[j, 0, t] = d
            dqkv_ref[j * L:(j + 1) * L, t * L:(t + 1) * L] = d

    def dw_step(r, carry):
        cols = pl.ds(pl.multiple_of(r * QB, QB), QB)
        hc = hg_ref[:, 0, :, cols].reshape(S, QB)
        dwp_ref[cols, :] += dot_tn(hc, dqkv_ref[...])
        return carry

    lax.fori_loop(0, 4, dw_step, 0)
    dwp_ref[D:1025, :] += jnp.sum(dqkv_ref[...].astype(F32), axis=0, keepdims=True)


def attn_call(sel, hg, dog, w_qkv, b_qkv3):
    full = lambda b, s: (0, b, 0, 0)
    in_specs = [pl.BlockSpec((8, 1, QB, D), full), pl.BlockSpec((16, 1, L, L), full)]
    for t in R3:
        for u in range(2):
            in_specs.append(pl.BlockSpec((D, L), lambda b, s, t=t, u=u: (0, t * 8 + s[2 * u])))
    for t in R3:
        for u in range(2):
            in_specs.append(pl.BlockSpec((1, 8, L), lambda b, s, t=t, u=u: (t * 8 + s[2 * u], 0, 0)))
    flash = [pltpu.VMEM((QB, S), F32), pltpu.VMEM((QB, S), BF), pltpu.VMEM((QB, S), BF)]
    band = [pltpu.VMEM((QB, 768), F32), pltpu.VMEM((QB, 768), BF), pltpu.VMEM((QB, 768), BF)]
    return pl.pallas_call(
        attn_kernel,
        grid_spec=pltpu.PrefetchScalarGridSpec(
            num_scalar_prefetch=1,
            grid=(2,),
            in_specs=in_specs,
            out_specs=[
                pl.BlockSpec((N, 1, L, L), full),
                pl.BlockSpec((N, 1, 3, L, L), lambda b, s: (0, b, 0, 0, 0)),
                pl.BlockSpec((DR, W3), lambda b, s: (0, 0)),
            ],
            scratch_shapes=[
                pltpu.VMEM((D, W3), BF), pltpu.VMEM((8, W3), F32),
                pltpu.VMEM((S, W3), BF), pltpu.VMEM((S, W3), BF),
                pltpu.VMEM((L, S), BF), pltpu.VMEM((L, S), BF),
                pltpu.VMEM((L, S), F32), pltpu.VMEM((L, S), F32),
            ] + flash + band,
        ),
        out_shape=[jax.ShapeDtypeStruct((N, 2, L, L), BF), jax.ShapeDtypeStruct((N, 2, 3, L, L), BF),
                   jax.ShapeDtypeStruct((DR, W3), F32)],
        compiler_params=pltpu.CompilerParams(vmem_limit_bytes=VMEM_CAP, dimension_semantics=("arbitrary",)),
        cost_estimate=pl.CostEstimate(flops=40 * 10**9, bytes_accessed=20 << 20, transcendentals=0),
        name="attn",
    )(sel, hg, dog, *([w_qkv] * 6), *([b_qkv3] * 6))


def gather_heads(recv_at, pos, b, m):
    pa, pb = pos[2 * m], pos[2 * m + 1]
    k, j = b // 2, b % 2
    a = recv_at(2 * (pa % 8) + k, j)
    c = recv_at(2 * (pb % 8) + k, j)
    return pair_halves(a, pa // 8, c, pb // 8)


def post_kernel(kind_ref, so_hbm, sd_hbm, dwp_ref, x_ref, dy_ref, gamma_ref, bout_ref, wqkv_hbm, wout_hbm,
                y_ref, dx_ref, small_ref, dwg_ref, dwo_ref,
                ro_ref, rd_ref, o_ref, dqkv_ref, wqkv_ref, wout_ref, dwx_ref, dws_ref, part_ref, px_ref, acc_ref,
                rs0_ref, rs1_ref, rs2_ref, sm_ref,
                loc, o_send, o_recv, d_send, d_recv, s_send, s_recv, x_send, x_recv,
                w_send, w_recv, g_send, g_recv, ws_send, ws_recv, gs_send, gs_recv, r_send, r_recv):
    pc = Place()
    barrier_signal(pc)
    loads = [pltpu.make_async_copy(so_hbm.at[pc.me], ro_ref.at[pc.me], loc.at[0]),
             pltpu.make_async_copy(sd_hbm.at[pc.me], rd_ref.at[pc.me], loc.at[1]),
             pltpu.make_async_copy(wout_hbm, wout_ref, loc.at[2]),
             pltpu.make_async_copy(wqkv_hbm, wqkv_ref, loc.at[3])]
    for cp in loads:
        cp.start()
    pos = head_places(kind_ref)
    gamma = gamma_ref[...].reshape(1, D).astype(F32)
    bout = bout_ref[...].reshape(1, D).astype(F32)
    barrier_wait()
    sends = exchange(pc, lambda t: so_hbm.at[t], lambda t: ro_ref.at[t], o_send, o_recv)
    half = rcopy(dwp_ref.at[1 - pc.core], dwx_ref, x_send.at[0], x_recv.at[0], pc.sib)
    half.start()
    sends += exchange(pc, lambda t: sd_hbm.at[t], lambda t: rd_ref.at[t], d_send, d_recv)
    half.wait_recv()
    dws_ref[...] = dwp_ref[pc.core] + dwx_ref[...]

    def w_rows(p):
        return pl.ds(W_ROWS[p], W_ROWS[p + 1] - W_ROWS[p])

    def o_rows(p):
        return pl.ds(O_ROWS[p], O_ROWS[p + 1] - O_ROWS[p])

    def w_slot(c, p, core=pc.core):
        return dwg_ref.at[c, core, w_rows(p)]

    def g_slot(c, p, core=pc.core):
        return dwo_ref.at[core, c, o_rows(p)]

    def to_sib(n, src, dst, send, recv):
        cp = rcopy(src, dst, send.at[n], recv.at[n], pc.sib)
        cp.start()
        sends.append(cp)

    wtree = Tree(pc, lambda p: dws_ref.at[w_rows(p)], w_slot, w_send, w_recv)
    wtree.start_own()
    keep_w = pltpu.make_async_copy(dws_ref, dwg_ref.at[pc.chip, pc.core], loc.at[4])
    keep_w.start()
    for p in R3:
        to_sib(p, dws_ref.at[w_rows(p)], w_slot(pc.chip, p), ws_send, ws_recv)

    def w_arrive(s):
        for e in wtree.level(s):
            c, p = wtree.arrive(e)
            to_sib(3 + wtree.entries.index(e), w_slot(c, p), w_slot(c, p), ws_send, ws_recv)

    loads[0].wait()
    loads[2].wait()
    exchange_wait(pc, lambda t: ro_ref.at[t], o_send, o_recv)
    for b in R4:
        for m in R8:
            o_ref[b * L:(b + 1) * L, m * L:(m + 1) * L] = gather_heads(lambda q, j: ro_ref[q, j], pos, b, m)
    dy_all = dy_ref[...].reshape(T, D)
    for c in R4:
        part_ref[c // 2, c % 2 * QB:(c % 2 + 1) * QB] = dot_tn(o_ref[:, c * QB:(c + 1) * QB], dy_all)
    dbo = jnp.zeros((1, D), F32)
    for b in R4:
        rows = slice(b * L, (b + 1) * L)
        xf = x_ref[b].astype(F32)
        y_ref[b] = (xf + dot_nn(o_ref[rows], wout_ref[...]) + bout).astype(BF)
        dbo += jnp.sum(dy_ref[b].astype(F32), axis=0, keepdims=True)
    xp = rcopy(part_ref.at[1 - pc.core], px_ref, x_send.at[1], x_recv.at[1], pc.sib)
    xp.start()
    xp.wait_recv()
    acc_ref[...] = (part_ref[pc.core] + px_ref[...]).reshape(8, 64, D)

    bufs = (rs0_ref, rs1_ref, rs2_ref)

    def reduce_step(s, wait):
        for p in R3:
            order = [(p + j) % 3 for j in R3]
            for i, sub in enumerate(subsets(order[s + 1:])):
                n = p * 7 + (0, 4, 6)[s] + i
                dst = bufs[s].at[i, o_rows(p)]
                if not wait:
                    cp = rcopy(acc_ref.at[pc.chip_at((order[s],) + sub), o_rows(p)], dst,
                               r_send.at[n], r_recv.at[n], pc.next_dev(order[s]))
                    cp.start()
                    sends.append(cp)
                else:
                    rcopy(dst, dst, r_send.at[n], r_recv.at[n], pc.sib).wait_recv()
                    acc_ref[pc.chip_at(sub), o_rows(p)] += bufs[s][i, o_rows(p)]

    reduce_step(0, False)
    loads[1].wait()
    loads[3].wait()
    exchange_wait(pc, lambda t: rd_ref.at[t], d_send, d_recv)
    w_arrive(0)
    for b in R4:
        for m in R8:
            for t in R3:
                dqkv_ref[b * L:(b + 1) * L, t * D + m * L:t * D + (m + 1) * L] = gather_heads(
                    lambda q, j: rd_ref[q, j, t], pos, b, m)
    reduce_step(0, True)
    reduce_step(1, False)
    dg = jnp.zeros((1, D), F32)
    db = jnp.zeros((1, D), F32)
    for b in R4:
        rows = slice(b * L, (b + 1) * L)
        xf = x_ref[b].astype(F32)
        cen = xf - jnp.mean(xf, axis=-1, keepdims=True)
        rstd = lax.rsqrt(jnp.mean(cen * cen, axis=-1, keepdims=True) + LN_EPS)
        xhat = cen * rstd
        dh = dot_nt(dqkv_ref[rows], wqkv_ref[...]).astype(BF).astype(F32)
        dg += jnp.sum(dh * xhat, axis=0, keepdims=True)
        db += jnp.sum(dh, axis=0, keepdims=True)
        dxh = dh * gamma
        m1 = jnp.mean(dxh, axis=-1, keepdims=True)
        m2 = jnp.mean(dxh * xhat, axis=-1, keepdims=True)
        dx_ref[b] = (dy_ref[b].astype(F32) + rstd * (dxh - m1 - xhat * m2)).astype(BF)
    row = lax.broadcasted_iota(jnp.int32, (8, D), 0)
    sm_ref[pc.me] = jnp.where(row == 0, dg, jnp.where(row == 1, db, jnp.where(row == 2, dbo, 0.0)))
    w_arrive(1)
    reduce_step(1, True)
    reduce_step(2, False)
    sends += exchange(pc, lambda t: sm_ref.at[pc.me], lambda t: sm_ref.at[t], s_send, s_recv)
    reduce_step(2, True)
    gtree = Tree(pc, lambda p: acc_ref.at[pc.chip, o_rows(p)], g_slot, g_send, g_recv)
    gtree.start_own()
    keep_g = pltpu.make_async_copy(acc_ref.at[pc.chip], dwo_ref.at[pc.core, pc.chip], loc.at[5])
    keep_g.start()
    for p in R3:
        to_sib(p, acc_ref.at[pc.chip, o_rows(p)], g_slot(pc.chip, p), gs_send, gs_recv)

    def g_arrive(s):
        for e in gtree.level(s):
            c, p = gtree.arrive(e)
            to_sib(3 + gtree.entries.index(e), g_slot(c, p), g_slot(c, p), gs_send, gs_recv)

    w_arrive(2)
    g_arrive(0)
    exchange_wait(pc, lambda t: sm_ref.at[t], s_send, s_recv)
    tot = sm_ref[0]
    for n in range(1, N):
        tot = tot + sm_ref[n]
    small_ref[...] = tot
    g_arrive(1)
    g_arrive(2)
    for tree, slot, send, recv in ((wtree, w_slot, ws_send, ws_recv), (gtree, g_slot, gs_send, gs_recv)):
        for p in R3:
            at = slot(pc.chip, p, 1 - pc.core)
            rcopy(at, at, send.at[p], recv.at[p], pc.sib).wait_recv()
        for i, (p, axis, sub) in enumerate(tree.entries):
            at = slot(pc.chip_at(sub + (axis,)), p, 1 - pc.core)
            rcopy(at, at, send.at[3 + i], recv.at[3 + i], pc.sib).wait_recv()
        tree.finish()
    for cp in sends + [half, xp]:
        cp.wait_send()
    keep_w.wait()
    keep_g.wait()


def post_call(kind, so, sd, dwp, x, dy, gamma, bout, wqkv, wout):
    vm, sm, hb = (pl.BlockSpec(memory_space=m) for m in (pltpu.VMEM, pltpu.SMEM, pl.ANY))
    sem = pltpu.SemaphoreType.DMA
    tok = jax.ShapeDtypeStruct((4, L, D), BF)
    pair = lambda n: [sem((n,)), sem((n,))]
    return pl.pallas_call(
        post_kernel,
        out_shape=(tok, tok, jax.ShapeDtypeStruct((8, D), F32), jax.ShapeDtypeStruct((8, 2, HR, W3), F32),
                   jax.ShapeDtypeStruct((2, 8, 64, D), F32)),
        in_specs=[sm, hb, hb] + [vm] * 5 + [hb, hb],
        out_specs=(vm, vm, vm, hb, hb),
        scratch_shapes=[
            pltpu.VMEM((N, 2, L, L), BF), pltpu.VMEM((N, 2, 3, L, L), BF),
            pltpu.VMEM((T, D), BF), pltpu.VMEM((T, D3), BF), pltpu.VMEM((D, D3), BF), pltpu.VMEM((D, D), BF),
            pltpu.VMEM((HR, W3), F32), pltpu.VMEM((HR, W3), F32),
            pltpu.VMEM((2, T, D), F32), pltpu.VMEM((T, D), F32), pltpu.VMEM((8, 64, D), F32),
            pltpu.VMEM((4, 64, D), F32), pltpu.VMEM((2, 64, D), F32), pltpu.VMEM((1, 64, D), F32),
            pltpu.VMEM((N, 8, D), F32), sem((6,))]
        + pair(N) + pair(N) + pair(N) + pair(2) + pair(21) + pair(21) + pair(24) + pair(24) + pair(21),
        compiler_params=pltpu.CompilerParams(vmem_limit_bytes=VMEM_CAP, collective_id=1, has_side_effects=True),
        name="post",
    )(kind, so, sd, dwp, x, dy, gamma, bout, wqkv, wout)


def unpack_kernel(kind_ref, dw_ref, bias_in_ref, dwo_ref, small_ref, out_ref, bias_ref, wo_ref, dg_ref, db_ref, dbo_ref):
    pos = head_places(kind_ref)
    wo_ref[...] = dwo_ref[...]

    def pick(ref, t, m):
        cols = slice(t * L, (t + 1) * L)
        pa, pb = pos[2 * m], pos[2 * m + 1]
        return pair_halves(ref[pa % 8, :, cols], pa // 8, ref[pb % 8, :, cols], pb // 8)

    for t in R3:
        for m in R8:
            out_ref[:, t * D + m * L:t * D + (m + 1) * L] = pick(dw_ref, t, m)

    @pl.when(pl.program_id(0) == 0)
    def _():
        for t in R3:
            for m in R8:
                bias_ref[t * D + m * L:t * D + (m + 1) * L] = pick(bias_in_ref, t, m)[0]
        dg_ref[...] = small_ref[0]
        db_ref[...] = small_ref[1]
        dbo_ref[...] = small_ref[2]


def unpack_call(kind, dwg, dwo, small):
    vec = jax.ShapeDtypeStruct((D,), F32)
    one = lambda r, s: (0,)
    return pl.pallas_call(
        unpack_kernel,
        grid_spec=pltpu.PrefetchScalarGridSpec(
            num_scalar_prefetch=1,
            grid=(8,),
            in_specs=[pl.BlockSpec((8, L, W3), lambda r, s: (0, r, 0)), pl.BlockSpec((8, 8, W3), lambda r, s: (0, L, 0)),
                      pl.BlockSpec((L, D), lambda r, s: (r, 0)), pl.BlockSpec((8, D), lambda r, s: (0, 0))],
            out_specs=[pl.BlockSpec((L, D3), lambda r, s: (r, 0)), pl.BlockSpec((D3,), one),
                       pl.BlockSpec((L, D), lambda r, s: (r, 0))] + [pl.BlockSpec((D,), one)] * 3,
        ),
        out_shape=[jax.ShapeDtypeStruct((D, D3), F32), jax.ShapeDtypeStruct((D3,), F32),
                   jax.ShapeDtypeStruct((D, D), F32), vec, vec, vec],
        compiler_params=pltpu.CompilerParams(vmem_limit_bytes=VMEM_CAP),
        name="unpack",
    )(kind, dwg, dwg, dwo, small)


def solution(mesh):
    tok_spec = P(None, "sp", None)

    def local_block(x, d_y, ln_gamma, ln_beta, w_qkv, b_qkv, w_out, b_out, head_kind):
        hg, dog, sel = pre_call(head_kind, x, d_y, ln_gamma, ln_beta, w_out.reshape(N, 64, D))
        b3 = jnp.broadcast_to(b_qkv.reshape(24, 1, L), (24, 8, L))
        so, sd, dwp = attn_call(sel, hg.reshape(8, 2, QB, D), dog, w_qkv, b3)
        y, dx, small, dwg, dwo = post_call(
            head_kind, so, sd, dwp.reshape(2, HR, W3), x, d_y, ln_gamma, b_out, w_qkv, w_out)
        dw, dbias, dwout, dg, db, dbo = unpack_call(head_kind, dwg.reshape(8, DR, W3), dwo.reshape(D, D), small)
        return y, dx, dg, db, dw, dbias, dwout, dbo

    return jax.shard_map(
        local_block, mesh=mesh,
        in_specs=(tok_spec, tok_spec, P(), P(), P(), P(), P(), P(), P()),
        out_specs=(tok_spec, tok_spec, P(), P(), P(), P(), P(), P()), check_vma=False)
```

time: 406 us -> 293 us (0.72)
  waiting for transfers between devices: 196 us -> 0 us
  Pallas kernels: 103 us -> 289 us
  blocking collectives: 34.7 us -> 0 us
  local copies, waits for them, and re-layouts: 23.3 us -> 3.27 us
  other arithmetic: 19.5 us -> 0 us
  between operations: 19.1 us -> 0.68 us
  starting transfers between devices: 9.37 us -> 0 us
    pallas_call x2, Pallas kernels: 25.8 us -> 215 us  [the longest x1 138 us: post_call(): pl.pallas_call(post_kernel, out_shape=(tok, tok, jax.ShapeDtypeStruct((8,...]
    all_to_all x2 -> x0, waiting for transfers between devices: 79.6 us -> none  [the longest x1 62.6 us: local_block(): recv = lax.all_to_all(send, 'sp', 0, 0, tiled=True)]
    all_gather x2 -> x0, waiting for transfers between devices: 78.3 us -> none  [the longest x1 55.1 us: local_block(): lax.all_gather(blk, 'sp', axis_index_groups=[list(range(0, 16, 2)), list(...]
    psum x1 -> x0, waiting for transfers between devices: 36.2 us -> none  [local_block(): dwout, small = lax.psum((dwout, small), 'sp')]
    psum x1 -> x0, blocking collectives: 34.7 us -> none  [local_block(): dwout, small = lax.psum((dwout, small), 'sp')]
    add x2 -> x0, other arithmetic: 14.7 us -> none  [the longest x1 14 us: local_block(): dw = unpack_call(pos, dwg[:, 0] + dwg[:, 1])]
    slice x3 -> x0, local copies, waits for them, and re-layouts: 13.1 us -> none  [local_block(): return (y, dx, small[0], small[1], dw[:D], dw[D], dwout, small[2])]
    all_to_all x2 -> x0, starting transfers between devices: 8.47 us -> none  [the longest x1 4.93 us: local_block(): dog = lax.all_to_all(do.reshape(16, 2, L, L), 'sp', 0, 0, tiled=True)]
  transfers between devices with their start and end apart: 6 -> 0, of which waited for: 6 -> 0; matrix products, arithmetic and copies ran while one was open for 7% -> 0% of each run, Pallas kernels for 10% -> 0%
where the time goes in v2:
time: 293 us
  Pallas kernels  289 us (99%)
  local copies, waits for them, and re-layouts  3.27 us (1%)
    pallas_call x1, Pallas kernels, post_call(): pl.pallas_call(post_kernel, out_shape=(tok, tok, jax.ShapeDtypeStruct((8,...  138 us
    pallas_call x1, Pallas kernels, pre_call(): pl.pallas_call(pre_kernel, out_shape=(jax.ShapeDtypeStruct((8, T, D), BF)...  76.8 us
    pallas_call x1, Pallas kernels, attn_call(): pl.pallas_call(attn_kernel, grid_spec=pltpu.PrefetchScalarGridSpec(num_sc...  57 us
    pallas_call x1, Pallas kernels, unpack_call(): pl.pallas_call(unpack_kernel, grid_spec=pltpu.PrefetchScalarGridSpec(num_...  17.5 us

profile of v2, /device:TPU:0, one launch (start us, length us, event | category | flops | bytes accessed | tf_op | source)
XLA Modules:
  0.0 293.1 jit_solution(10098148515403807047)
XLA Ops:
  0.6 1.3 broadcast_in_dim.8.refs_6_.refs_7_.refs_8_.refs_9_.refs_10_.refs_11_
  2.0 76.8 %pre.1 = (bf16[8,512,1024]{2,1,0:T(8,128)(2,1)}, bf16[16,2,128,128]{3,2,1,0:T(8,128)(2,1)}, s32[4]{0:T(128)}) custom-call(s32[16]{0:T(128)} %kind_ref.5, bf16[4,128,1024]{2,1,0:T(8,128)(2,1)} %x_ref.3, bf16[4,128,1024]{2,1,0:T(8,128)(2,1)} %dy_ref.3, bf16[1024]{0:T(1024)(128)(2,1)} %gamma_ref.3, bf16[1024]{0:T(1024)(128)(2,1)} %beta_ref.1, ...), custom_call_target="tpu_custom_call" | custom-call | tf_op jit(solution)/shard_map/pre/pallas_call | solution.py:238
  78.7 57.0 %attn.1 = (bf16[16,2,128,128]{3,2,1,0:T(8,128)(2,1)}, bf16[16,2,3,128,128]{4,3,2,1,0:T(8,128)(2,1)}, f32[1040,384]{1,0:T(8,128)}) custom-call(s32[4]{0:T(128)} %get-tuple-element.25.sel_ref, bf16[8,2,256,1024]{3,2,1,0:T(8,128)(2,1)} %bitcast.12, bf16[16,2,128,128]{3,2,1,0:T(8,128)(2,1)} %get-tuple-element.27.dog_ref, bf16[1024,3072]{1,0:T(8,128)(2,1)} %wqkv_hbm.1, ...), custom_call_target="tpu_custom_call" | custom-call | flops 40000000000 | bytes 20971520 | tf_op jit(solution)/shard_map/attn/pallas_call | solution.py:379
  135.8 137.8 %post.1 = (bf16[4,128,1024]{2,1,0:T(8,128)(2,1)}, bf16[4,128,1024]{2,1,0:T(8,128)(2,1)}, f32[8,1024]{1,0:T(8,128)}, f32[8,2,520,384]{3,2,1,0:T(8,128)}, f32[2,8,64,1024]{3,2,1,0:T(8,128)}) custom-call(s32[16]{0:T(128)} %kind_ref.5, bf16[16,2,128,128]{3,2,1,0:T(8,128)(2,1)} %get-tuple-element.28.so_hbm, ...), custom_call_target="tpu_custom_call" | custom-call | tf_op jit(solution)/shard_map/post/pallas_call | solution.py:578
  273.6 0.0 copy-start.1
  273.6 0.0 copy-start
  273.6 17.5 %unpack.1 = (f32[1024,3072]{1,0:T(8,128)}, f32[3072]{0:T(1024)}, f32[1024,1024]{1,0:T(8,128)}, f32[1024]{0:T(1024)}, f32[1024]{0:T(1024)}, /*index=5*/f32[1024]{0:T(1024)}) custom-call(s32[16]{0:T(128)} %kind_ref.5, f32[8,1040,384]{2,1,0:T(8,128)} %bitcast.6, f32[8,1040,384]{2,1,0:T(8,128)} %bitcast.7, f32[1024,1024]{1,0:T(8,128)} %bitcast.9, ...), custom_call_target="tpu_custom_call" | custom-call | tf_op jit(solution)/shard_map/unpack/pallas_call | solution.py:623
  291.2 0.0 copy-done.1
  291.2 1.0 copy.19
  292.2 0.0 copy-done
  292.2 1.0 copy.20
Async XLA Ops:
  273.6 17.6 %copy-start.1 = (bf16[4,128,1024]{2,1,0:T(8,128)(2,1)S(1)}, bf16[4,128,1024]{2,1,0:T(8,128)(2,1)}, u32[]{:S(2)}) copy-start(bf16[4,128,1024]{2,1,0:T(8,128)(2,1)} %get-tuple-element.50) | copy-start | bytes 3145732
  273.6 18.5 %copy-start = (bf16[4,128,1024]{2,1,0:T(8,128)(2,1)S(1)}, bf16[4,128,1024]{2,1,0:T(8,128)(2,1)}, u32[]{:S(2)}) copy-start(bf16[4,128,1024]{2,1,0:T(8,128)(2,1)} %get-tuple-element.51) | copy-start | bytes 3145732

commit v3 on v2

v3 whole, which is shorter than its diff:
```python
import functools
import math

import jax
import jax.numpy as jnp
from jax import lax
from jax.experimental import pallas as pl
from jax.experimental.pallas import tpu as pltpu
from jax.sharding import PartitionSpec as P

LN_EPS = 1e-5
NEG_BIG = -1e30
BF = jnp.bfloat16
F32 = jnp.float32
QB = 256
L = 128
W3 = 384
T = 512
D = 1024
DR = 1040
HR = 520
N = 16
R3, R4, R8 = range(3), range(4), range(8)
MESH = pl.DeviceIdType.MESH
H_ROWS = (0, 96, 176, 256)
W_ROWS = (0, 176, 352, 520)
O_ROWS = (0, 24, 48, 64)
S = 2048
D3 = 3072
VMEM_CAP = 63 * D * D


def dot_nn(a, b):
    return lax.dot_general(a, b, (((1,), (0,)), ((), ())), preferred_element_type=F32)


def dot_nt(a, b):
    return lax.dot_general(a, b, (((1,), (1,)), ((), ())), preferred_element_type=F32)


def dot_tn(a, b):
    return lax.dot_general(a, b, (((0,), (0,)), ((), ())), preferred_element_type=F32)


def swap_halves(a):
    return jnp.concatenate([a[:, 64:], a[:, :64]], axis=1)


def pair_halves(a, a_half, b, b_half):
    lane = lax.broadcasted_iota(jnp.int32, a.shape, 1)
    a = jnp.where(a_half == 1, swap_halves(a), a)
    b = jnp.where(b_half == 0, swap_halves(b), b)
    return jnp.where(lane < 64, a, b)


class Place:
    def __init__(self):
        self.me = lax.axis_index("sp")
        self.core, self.chip = self.me % 2, self.me // 2
        self.sib = self.me + 1 - 2 * self.core
        bits = (self.chip % 2, self.chip // 2 % 2, self.chip // 4)
        self.step = [(1 - 2 * v) * w for v, w in zip(bits, (1, 2, 4))]

    def chip_at(self, axes):
        out = self.chip
        for a in axes:
            out = out + self.step[a]
        return out

    def next_dev(self, axis):
        return self.me + 2 * self.step[axis]


def rcopy(src, dst, send, recv, dev):
    return pltpu.make_async_remote_copy(
        src_ref=src, dst_ref=dst, send_sem=send, recv_sem=recv, device_id=(dev,), device_id_type=MESH)


def subsets(axes):
    out = [()]
    for a in axes:
        out += [v + (a,) for v in out]
    return out


class Tree:
    def __init__(self, place, own, slot, send, recv):
        self.place, self.own, self.slot, self.send, self.recv = place, own, slot, send, recv
        self.entries = []
        for s in R3:
            for p in R3:
                order = [(p + j) % 3 for j in R3]
                for sub in subsets(order[:s]):
                    self.entries.append((p, order[s], sub))

    def copy(self, e):
        p, axis, sub = e
        i = self.entries.index(e)
        at = self.slot(self.place.chip_at(sub), p)
        return rcopy(at if sub else self.own(p), at, self.send.at[i], self.recv.at[i], self.place.next_dev(axis))

    def start_own(self):
        for e in self.entries:
            if not e[2]:
                self.copy(e).start()

    def arrive(self, e):
        p, axis, sub = e
        got = sub + (axis,)
        chip = self.place.chip_at(got)
        at = self.slot(chip, p)
        i = self.entries.index(e)
        rcopy(at, at, self.send.at[i], self.recv.at[i], self.place.next_dev(axis)).wait_recv()
        for n in self.entries:
            if n[0] == p and n[2] == got:
                self.copy(n).start()
        return chip, p

    def level(self, s):
        return [e for e in self.entries if len(e[2]) <= s and (e[1] - e[0]) % 3 == s]

    def finish(self):
        for e in self.entries:
            self.copy(e).wait_send()


def barrier_signal(place):
    sem = pltpu.get_barrier_semaphore()
    for r in range(1, N):
        pl.semaphore_signal(sem, inc=1, device_id=((place.me + r) % N,), device_id_type=MESH)


def barrier_wait():
    pl.semaphore_wait(pltpu.get_barrier_semaphore(), N - 1)


def head_places(kind_ref):
    pos, zeros, ones = [], 0, 8
    for n in range(N):
        k = kind_ref[n]
        pos.append(jnp.where(k == 0, zeros, ones))
        zeros, ones = zeros + 1 - k, ones + k
    return pos


class Exchange:
    def __init__(self, place, src, dst, send, recv):
        self.place, self.src, self.dst, self.send, self.recv = place, src, dst, send, recv

    def copies(self):
        me = self.place.me
        for r in range(1, N):
            to = (me + r) % N
            yield rcopy(self.src(to), self.dst(me), self.send(r), self.recv(r), to)

    def start(self):
        for cp in self.copies():
            cp.start()

    def wait(self):
        for r in range(1, N):
            at = self.dst((self.place.me + N - r) % N)
            rcopy(at, at, self.send(r), self.recv(r), self.place.me).wait_recv()

    def finish(self):
        for cp in self.copies():
            cp.wait_send()


def gather_heads(recv_at, pos, b, m):
    pa, pb = pos[2 * m], pos[2 * m + 1]
    k, j = b // 2, b % 2
    a = recv_at(j, 2 * (pa % 8) + k)
    c = recv_at(j, 2 * (pb % 8) + k)
    return pair_halves(a, pa // 8, c, pb // 8)


def span(tab):
    return lambda p: pl.ds(tab[p], tab[p + 1] - tab[p])


def centre(xb):
    xf = xb.astype(F32)
    cen = xf - jnp.mean(xf, axis=-1, keepdims=True)
    rstd = lax.rsqrt(jnp.mean(cen * cen, axis=-1, keepdims=True) + LN_EPS)
    return xf, cen * rstd, rstd


def layer_kernel(kind_ref, x_ref, dy_ref, gamma_ref, beta_ref, bout_ref, b3_ref, wqkv_hbm, wout_hbm,
                 y_ref, dx_ref, small_ref, dwg_ref, dwo_ref,
                 hg_ref, out_ref, wout_ref, wp_ref, do_ref, dog_ref, w_ref, bias_ref, qkv_ref, dqkv_ref, qt_ref, dot_ref,
                 dkt_ref, dvt_ref, s_f, p_f, ds_f, s_g, p_g, ds_g, so_ref, sd_ref, ro_ref, rd_ref, o_nat, dqkv_nat,
                 dwp_ref, dws_ref, part_ref, px_ref, acc_ref, rs0_ref, rs1_ref, rs2_ref, sm_ref,
                 loc, sib_send, sib_recv, h_send, h_recv, do_send, do_recv, o_send, o_recv, d_send, d_recv,
                 s_send, s_recv, w_send, w_recv, g_send, g_recv, ws_send, ws_recv, gs_send, gs_recv, r_send, r_recv):
    pc = Place()
    barrier_signal(pc)

    def w_load(r):
        return pltpu.make_async_copy(wqkv_hbm.at[r * T:(r + 1) * T], dqkv_nat, loc.at[r])

    wo_load = pltpu.make_async_copy(wout_hbm, wout_ref, loc.at[2])
    w_load(0).start()
    wo_load.start()
    gamma = gamma_ref[...].reshape(1, D).astype(F32)
    beta = beta_ref[...].reshape(1, D).astype(F32)
    bout = bout_ref[...].reshape(1, D).astype(F32)

    def rows_of(core):
        return pl.ds(pl.multiple_of(core * L, L), L)

    def norm(xb):
        return (centre(xb)[1] * gamma + beta).astype(BF)

    def sib_copy(j):
        return rcopy(out_ref.at[j], hg_ref.at[pc.chip, j, rows_of(pc.core)], sib_send.at[j], sib_recv.at[j], pc.sib)

    for j in range(2):
        out_ref[j] = norm(x_ref[2 * (1 - pc.core) + j])
    for j in range(2):
        hg_ref[pc.chip, j, rows_of(pc.core)] = norm(x_ref[2 * pc.core + j])
    barrier_wait()
    for j in range(2):
        sib_copy(j).start()

    h_rows, w_rows, o_rows = span(H_ROWS), span(W_ROWS), span(O_ROWS)

    def h_tree(j):
        slot = lambda c, p: hg_ref.at[c, j, h_rows(p)]
        return Tree(pc, lambda p: slot(pc.chip, p), slot, h_send.at[j], h_recv.at[j])

    def sib_arrive(j):
        at = hg_ref.at[pc.chip, j, rows_of(1 - pc.core)]
        rcopy(at, at, sib_send.at[j], sib_recv.at[j], pc.sib).wait_recv()

    do_out = do_ref.reshape(N, 2, L, L)

    def swap(src, dst, send, recv, j):
        return Exchange(pc, lambda t: src(t, j), lambda t: dst.at[j, t], lambda r: send.at[j, r], lambda r: recv.at[j, r])

    def do_swap(j):
        return swap(lambda t, j: do_out.at[t, j], dog_ref, do_send, do_recv, j)

    def o_swap(j):
        return swap(lambda t, j: so_ref.at[j, t], ro_ref, o_send, o_recv, j)

    def d_swap(j):
        return swap(lambda t, j: sd_ref.at[j, t], rd_ref, d_send, d_recv, j)

    trees = [h_tree(0), h_tree(1)]
    sib_arrive(0)
    trees[0].start_own()
    pos = head_places(kind_ref)
    perm = []
    for j in range(N):
        v = 0
        for n in range(1, N):
            v = v + jnp.where(pos[n] == j, n, 0)
        perm.append(v)
    f = g = 0
    for c in R8:
        f = f + jnp.where(pc.chip == c, perm[c], 0)
        g = g + jnp.where(pc.chip == c, perm[8 + c], 0)
    wo_load.wait()
    dy_all = dy_ref[...].reshape(T, D)
    for c in R4:
        for u in range(2):
            wp_ref[u * L:u * L + 64] = wout_ref[perm[2 * c + u]]
            wp_ref[u * L + 64:u * L + L] = wout_ref[perm[8 + 2 * c + u]]
        d = dot_nt(dy_all, wp_ref[...]).astype(BF)
        for u in range(2):
            do_ref[2 * c + u] = d[:, u * L:(u + 1) * L].reshape(4, L, L)
    for e in trees[0].level(0):
        trees[0].arrive(e)
    do_swap(0).start()
    for j in range(2):
        dog_ref[j, pc.me] = do_out[pc.me, j]

    def w_cols(t, k, head):
        out = None
        for m in R8:
            cur = dqkv_nat[k * L:(k + 1) * L, t * D + m * L:t * D + (m + 1) * L]
            out = cur if out is None else jnp.where(head // 2 == m, cur, out)
        return out

    for r in range(2):
        w_load(r).wait()
        for t in R3:
            for k in R4:
                w_ref[r * T + k * L:r * T + (k + 1) * L, t * L:(t + 1) * L] = pair_halves(
                    w_cols(t, k, f), f % 2, w_cols(t, k, g), g % 2)
        if r == 0:
            w_load(1).start()
    for t in R3:
        bias_ref[:, t * L:(t + 1) * L] = pair_halves(
            b3_ref[t * 8 + f // 2].astype(F32), f % 2, b3_ref[t * 8 + g // 2].astype(F32), g % 2)
    dwp_ref[...] = jnp.zeros_like(dwp_ref)
    for e in trees[0].level(1):
        trees[0].arrive(e)
    sib_arrive(1)
    trees[1].start_own()
    for e in trees[0].level(2):
        trees[0].arrive(e)
    do_swap(0).wait()

    lane = lax.broadcasted_iota(jnp.int32, (QB, L), 1)
    row_i = lax.broadcasted_iota(jnp.int32, (QB, QB), 0)
    col_i = lax.broadcasted_iota(jnp.int32, (QB, QB), 1)

    def head_block(j, i, hd):
        s_ref, p_ref, ds_ref = ((s_f, p_f, ds_f), (s_g, p_g, ds_g))[hd]
        first = 0 if hd == 0 else max(0, i - 2)
        blocks = range(first, i + 1)
        mine = (lane < 64) if hd == 0 else (lane >= 64)
        qi = qkv_ref[i * QB:(i + 1) * QB, 0:L] * BF(0.125)
        doi = dog_ref[j, 2 * i:2 * i + 2].reshape(QB, L)
        qm = jnp.where(mine, qi, BF(0))
        dom = jnp.where(mine, doi, BF(0))
        k_at = lambda kb: qkv_ref[kb * QB:(kb + 1) * QB, L:2 * L]
        v_at = lambda kb: qkv_ref[kb * QB:(kb + 1) * QB, 2 * L:3 * L]
        at = lambda kb: slice((kb - first) * QB, (kb - first + 1) * QB)
        mx = None
        for kb in blocks:
            s = dot_nt(qm, k_at(kb))
            if kb == i:
                s = jnp.where(col_i <= row_i, s, NEG_BIG)
            if hd == 1 and kb == i - 2:
                s = jnp.where(col_i > row_i, s, NEG_BIG)
            s_ref[:, at(kb)] = s
            cur = jnp.maximum(s[:, :L], s[:, L:])
            mx = cur if mx is None else jnp.maximum(mx, cur)
        m = jnp.max(mx, axis=1, keepdims=True)
        ls = None
        for kb in blocks:
            e = jnp.exp(s_ref[:, at(kb)] - m)
            s_ref[:, at(kb)] = e
            cur = e[:, :L] + e[:, L:]
            ls = cur if ls is None else ls + cur
        rl = 1.0 / jnp.sum(ls, axis=1, keepdims=True)
        acc = None
        for kb in blocks:
            p_ = s_ref[:, at(kb)] * rl
            s_ref[:, at(kb)] = p_
            pb = p_.astype(BF)
            p_ref[:, at(kb)] = pb
            cur = dot_nn(pb, v_at(kb))
            acc = cur if acc is None else acc + cur
        dsum = jnp.sum(dom.astype(F32) * acc, axis=1, keepdims=True)
        dq = None
        for kb in blocks:
            dp = dot_nt(dom, v_at(kb)).astype(BF).astype(F32)
            ds = (s_ref[:, at(kb)] * (dp - dsum)).astype(BF)
            ds_ref[:, at(kb)] = ds
            cur = dot_nn(ds, k_at(kb))
            dq = cur if dq is None else dq + cur
        hr = slice(hd * 64, hd * 64 + 64)
        n = len(blocks) * QB
        keys = slice(first * QB, first * QB + n)
        dvt_ref[hr, keys] += dot_nn(dot_ref[hr, i * QB:(i + 1) * QB], p_ref[:, :n])
        dkt_ref[hr, keys] += dot_nn(qt_ref[hr, i * QB:(i + 1) * QB], ds_ref[:, :n])
        return acc, dq * 0.125

    def batch_step(j, carry):
        def qkv_step(r, c):
            rows = hg_ref[pl.ds(2 * r, 2), j].reshape(T, D)
            out = dot_nn(rows, w_ref[...]) + bias_ref[0:1, :]
            qkv_ref[pl.ds(pl.multiple_of(r * T, T), T), :] = out.astype(BF)
            return c

        lax.fori_loop(0, 4, qkv_step, 0)

        @pl.when(j == 0)
        def _():
            for e in trees[1].level(0):
                trees[1].arrive(e)
            do_swap(1).start()

        for i in R8:
            qs = qkv_ref[i * QB:(i + 1) * QB, 0:L] * BF(0.125)
            qt_ref[:, i * QB:(i + 1) * QB] = qs.T
            dot_ref[:, i * QB:(i + 1) * QB] = dog_ref[j, 2 * i:2 * i + 2].reshape(QB, L).T
        dkt_ref[...] = jnp.zeros_like(dkt_ref)
        dvt_ref[...] = jnp.zeros_like(dvt_ref)
        for i in R8:
            of, dqf = head_block(j, i, 0)
            og, dqg = head_block(j, i, 1)
            o = jnp.where(lane < 64, of, og).astype(BF)
            dq = jnp.where(lane < 64, dqf, dqg).astype(BF)
            for u in range(2):
                so_ref[j, 2 * i + u] = o[u * L:(u + 1) * L]
                sd_ref[j, 2 * i + u, 0] = dq[u * L:(u + 1) * L]
            dqkv_ref[i * QB:(i + 1) * QB, 0:L] = dq
            if i == 4:
                @pl.when(j == 0)
                def _():
                    for e in trees[1].level(1):
                        trees[1].arrive(e)
        for t, src in ((1, dkt_ref), (2, dvt_ref)):
            for n in range(N):
                d = src[:, n * L:(n + 1) * L].T.astype(BF)
                sd_ref[j, n, t] = d
                dqkv_ref[n * L:(n + 1) * L, t * L:(t + 1) * L] = d
        o_swap(j).start()
        d_swap(j).start()
        ro_ref[j, pc.me] = so_ref[j, pc.me]
        rd_ref[j, pc.me] = sd_ref[j, pc.me]

        def dw_step(r, c):
            cols = pl.ds(pl.multiple_of(r * QB, QB), QB)
            dwp_ref[cols, :] += dot_tn(hg_ref[:, j, :, cols].reshape(S, QB), dqkv_ref[...])
            return c

        lax.fori_loop(0, 4, dw_step, 0)
        dwp_ref[D:D + 1, :] += jnp.sum(dqkv_ref[...].astype(F32), axis=0, keepdims=True)

        @pl.when(j == 0)
        def _():
            for e in trees[1].level(2):
                trees[1].arrive(e)
            do_swap(1).wait()

        return carry

    lax.fori_loop(0, 2, batch_step, 0)

    def half_of(core):
        return dwp_ref.at[pl.ds(pl.multiple_of(core * HR, 8), HR)]

    sends = []

    def to_sib(n, src, dst, send, recv):
        cp = rcopy(src, dst, send.at[n], recv.at[n], pc.sib)
        cp.start()
        sends.append(cp)
        return cp

    half = to_sib(2, half_of(1 - pc.core), dws_ref, sib_send, sib_recv)
    for j in range(2):
        trees[j].finish()
        do_swap(j).finish()
    w_flat = hg_ref.reshape(2 * S, D)
    w_loads = [pltpu.make_async_copy(wqkv_hbm.at[:, t * D:(t + 1) * D], w_flat.at[t * D:(t + 1) * D], loc.at[3 + t]) for t in R3]
    for cp in w_loads:
        cp.start()
    for j in range(2):
        o_swap(j).wait()
    for b in R4:
        for m in R8:
            o_nat[b * L:(b + 1) * L, m * L:(m + 1) * L] = gather_heads(lambda j, q: ro_ref[j, q], pos, b, m)

    def wout_part(core, c):
        cols = pl.ds(pl.multiple_of(core * T + c * QB, QB), QB)
        return dot_tn(o_nat[:, cols], dy_all)

    for c in range(2):
        part_ref[c * QB:(c + 1) * QB] = wout_part(1 - pc.core, c)
    xp = to_sib(3, part_ref, px_ref, sib_send, sib_recv)
    for c in range(2):
        acc_ref[4 * c:4 * c + 4] = wout_part(pc.core, c).reshape(4, 64, D)
    xp.wait_recv()
    acc_ref[...] += px_ref[...].reshape(8, 64, D)

    bufs = (rs0_ref, rs1_ref, rs2_ref)

    def reduce_step(s, wait):
        for p in R3:
            order = [(p + j) % 3 for j in R3]
            for i, sub in enumerate(subsets(order[s + 1:])):
                n = p * 7 + (0, 4, 6)[s] + i
                dst = bufs[s].at[i, o_rows(p)]
                if not wait:
                    cp = rcopy(acc_ref.at[pc.chip_at((order[s],) + sub), o_rows(p)], dst,
                               r_send.at[n], r_recv.at[n], pc.next_dev(order[s]))
                    cp.start()
                    sends.append(cp)
                else:
                    rcopy(dst, dst, r_send.at[n], r_recv.at[n], pc.sib).wait_recv()
                    acc_ref[pc.chip_at(sub), o_rows(p)] += bufs[s][i, o_rows(p)]

    reduce_step(0, False)
    half.wait_recv()
    dws_ref[...] += half_of(pc.core)[...]

    def w_slot(c, p, core=pc.core):
        return dwg_ref.at[c, core, w_rows(p)]

    def g_slot(c, p, core=pc.core):
        return dwo_ref.at[core, c, o_rows(p)]

    wtree = Tree(pc, lambda p: dws_ref.at[w_rows(p)], w_slot, w_send, w_recv)
    wtree.start_own()
    keep_w = pltpu.make_async_copy(dws_ref, dwg_ref.at[pc.chip, pc.core], loc.at[0])
    keep_w.start()
    for p in R3:
        to_sib(p, dws_ref.at[w_rows(p)], w_slot(pc.chip, p), ws_send, ws_recv)

    def pass_on(tree, slot, s, send, recv):
        for e in tree.level(s):
            c, p = tree.arrive(e)
            to_sib(3 + tree.entries.index(e), slot(c, p), slot(c, p), send, recv)

    dbo = jnp.zeros((1, D), F32)
    for b in R4:
        rows = slice(b * L, (b + 1) * L)
        y_ref[b] = (x_ref[b].astype(F32) + dot_nn(o_nat[rows], wout_ref.reshape(D, D)[...]) + bout).astype(BF)
        dbo += jnp.sum(dy_ref[b].astype(F32), axis=0, keepdims=True)
    for j in range(2):
        d_swap(j).wait()
    reduce_step(0, True)
    reduce_step(1, False)
    pass_on(wtree, w_slot, 0, ws_send, ws_recv)
    for b in R4:
        for m in R8:
            for t in R3:
                dqkv_nat[b * L:(b + 1) * L, t * D + m * L:t * D + (m + 1) * L] = gather_heads(
                    lambda j, q: rd_ref[j, q, t], pos, b, m)
    for cp in w_loads:
        cp.wait()
    reduce_step(1, True)
    reduce_step(2, False)
    dg = jnp.zeros((1, D), F32)
    db = jnp.zeros((1, D), F32)
    for b in R4:
        rows = slice(b * L, (b + 1) * L)
        _, xhat, rstd = centre(x_ref[b])
        dh = None
        for t in R3:
            cur = dot_nt(dqkv_nat[rows, t * D:(t + 1) * D], w_flat[t * D:(t + 1) * D])
            dh = cur if dh is None else dh + cur
        dh = dh.astype(BF).astype(F32)
        dg += jnp.sum(dh * xhat, axis=0, keepdims=True)
        db += jnp.sum(dh, axis=0, keepdims=True)
        dxh = dh * gamma
        m1 = jnp.mean(dxh, axis=-1, keepdims=True)
        m2 = jnp.mean(dxh * xhat, axis=-1, keepdims=True)
        dx_ref[b] = (dy_ref[b].astype(F32) + rstd * (dxh - m1 - xhat * m2)).astype(BF)
    row = lax.broadcasted_iota(jnp.int32, (8, D), 0)
    sm_ref[pc.me] = jnp.where(row == 0, dg, jnp.where(row == 1, db, jnp.where(row == 2, dbo, 0.0)))
    s_swap = Exchange(pc, lambda t: sm_ref.at[pc.me], lambda t: sm_ref.at[t], lambda r: s_send.at[r], lambda r: s_recv.at[r])
    s_swap.start()
    reduce_step(2, True)
    gtree = Tree(pc, lambda p: acc_ref.at[pc.chip, o_rows(p)], g_slot, g_send, g_recv)
    gtree.start_own()
    keep_g = pltpu.make_async_copy(acc_ref.at[pc.chip], dwo_ref.at[pc.core, pc.chip], loc.at[1])
    keep_g.start()
    for p in R3:
        to_sib(p, acc_ref.at[pc.chip, o_rows(p)], g_slot(pc.chip, p), gs_send, gs_recv)
    pass_on(wtree, w_slot, 1, ws_send, ws_recv)
    pass_on(gtree, g_slot, 0, gs_send, gs_recv)
    pass_on(gtree, g_slot, 1, gs_send, gs_recv)
    s_swap.wait()
    tot = sm_ref[0]
    for n in range(1, N):
        tot = tot + sm_ref[n]
    small_ref[...] = tot
    pass_on(wtree, w_slot, 2, ws_send, ws_recv)
    pass_on(gtree, g_slot, 2, gs_send, gs_recv)
    for tree, slot, send, recv in ((wtree, w_slot, ws_send, ws_recv), (gtree, g_slot, gs_send, gs_recv)):
        for p in R3:
            at = slot(pc.chip, p, 1 - pc.core)
            rcopy(at, at, send.at[p], recv.at[p], pc.sib).wait_recv()
        for i, (p, axis, sub) in enumerate(tree.entries):
            at = slot(pc.chip_at(sub + (axis,)), p, 1 - pc.core)
            rcopy(at, at, send.at[3 + i], recv.at[3 + i], pc.sib).wait_recv()
        tree.finish()
    for j in range(2):
        sib_copy(j).wait_send()
        o_swap(j).finish()
        d_swap(j).finish()
    s_swap.finish()
    for cp in sends:
        cp.wait_send()
    keep_w.wait()
    keep_g.wait()


def layer_call(kind, x, dy, gamma, beta, bout, b3, wqkv, wout):
    vm, sm, hb = (pl.BlockSpec(memory_space=m) for m in (pltpu.VMEM, pltpu.SMEM, pl.ANY))
    sem = pltpu.SemaphoreType.DMA
    tok = jax.ShapeDtypeStruct((4, L, D), BF)

    def pair(*n):
        return [sem(n), sem(n)]

    def bf(*n):
        return pltpu.VMEM(n, BF)

    def ff(*n):
        return pltpu.VMEM(n, F32)

    band = 3 * QB
    return pl.pallas_call(
        layer_kernel,
        out_shape=(tok, tok, jax.ShapeDtypeStruct((8, D), F32), jax.ShapeDtypeStruct((8, 2, HR, W3), F32),
                   jax.ShapeDtypeStruct((2, 8, 64, D), F32)),
        in_specs=[sm] + [vm] * 6 + [hb, hb],
        out_specs=(vm, vm, vm, hb, hb),
        scratch_shapes=[
            bf(8, 2, QB, D), bf(2, L, D), bf(N, 64, D), bf(QB, D), bf(8, 4, L, L), bf(2, N, L, L), bf(D, W3), ff(8, W3),
            bf(S, W3), bf(S, W3), bf(L, S), bf(L, S), ff(L, S), ff(L, S),
            ff(QB, S), bf(QB, S), bf(QB, S), ff(QB, band), bf(QB, band), bf(QB, band),
            bf(2, N, L, L), bf(2, N, 3, L, L), bf(2, N, L, L), bf(2, N, 3, L, L), bf(T, D), bf(T, D3),
            ff(DR, W3), ff(HR, W3), ff(T, D), ff(T, D), ff(8, 64, D),
            ff(4, 64, D), ff(2, 64, D), ff(1, 64, D), ff(N, 8, D), sem((6,))]
        + pair(4) + pair(2, 21) + pair(2, N) + pair(2, N) + pair(2, N) + pair(N)
        + pair(21) + pair(21) + pair(24) + pair(24) + pair(21),
        compiler_params=pltpu.CompilerParams(vmem_limit_bytes=VMEM_CAP, collective_id=0, has_side_effects=True),
        name="layer",
    )(kind, x, dy, gamma, beta, bout, b3, wqkv, wout)


def unpack_kernel(kind_ref, dw_ref, bias_in_ref, dwo_ref, small_ref, out_ref, bias_ref, wo_ref, dg_ref, db_ref, dbo_ref):
    pos = head_places(kind_ref)
    wo_ref[...] = dwo_ref[...]

    def pick(ref, t, m):
        cols = slice(t * L, (t + 1) * L)
        pa, pb = pos[2 * m], pos[2 * m + 1]
        return pair_halves(ref[pa % 8, :, cols], pa // 8, ref[pb % 8, :, cols], pb // 8)

    for t in R3:
        for m in R8:
            out_ref[:, t * D + m * L:t * D + (m + 1) * L] = pick(dw_ref, t, m)

    @pl.when(pl.program_id(0) == 0)
    def _():
        for t in R3:
            for m in R8:
                bias_ref[t * D + m * L:t * D + (m + 1) * L] = pick(bias_in_ref, t, m)[0]
        dg_ref[...] = small_ref[0]
        db_ref[...] = small_ref[1]
        dbo_ref[...] = small_ref[2]


def unpack_call(kind, dwg, dwo, small):
    vec = jax.ShapeDtypeStruct((D,), F32)
    one = lambda r, s: (0,)
    return pl.pallas_call(
        unpack_kernel,
        grid_spec=pltpu.PrefetchScalarGridSpec(
            num_scalar_prefetch=1,
            grid=(8,),
            in_specs=[pl.BlockSpec((8, L, W3), lambda r, s: (0, r, 0)), pl.BlockSpec((8, 8, W3), lambda r, s: (0, L, 0)),
                      pl.BlockSpec((L, D), lambda r, s: (r, 0)), pl.BlockSpec((8, D), lambda r, s: (0, 0))],
            out_specs=[pl.BlockSpec((L, D3), lambda r, s: (r, 0)), pl.BlockSpec((D3,), one),
                       pl.BlockSpec((L, D), lambda r, s: (r, 0))] + [pl.BlockSpec((D,), one)] * 3,
        ),
        out_shape=[jax.ShapeDtypeStruct((D, D3), F32), jax.ShapeDtypeStruct((D3,), F32),
                   jax.ShapeDtypeStruct((D, D), F32), vec, vec, vec],
        compiler_params=pltpu.CompilerParams(vmem_limit_bytes=VMEM_CAP),
        name="unpack",
    )(kind, dwg, dwg, dwo, small)


def solution(mesh):
    tok_spec = P(None, "sp", None)

    def local_block(x, d_y, ln_gamma, ln_beta, w_qkv, b_qkv, w_out, b_out, head_kind):
        b3 = jnp.broadcast_to(b_qkv.reshape(24, 1, L), (24, 8, L))
        y, dx, small, dwg, dwo = layer_call(head_kind, x, d_y, ln_gamma, ln_beta, b_out, b3, w_qkv, w_out.reshape(N, 64, D))
        dw, dbias, dwout, dg, db, dbo = unpack_call(head_kind, dwg.reshape(8, DR, W3), dwo.reshape(D, D), small)
        return y, dx, dg, db, dw, dbias, dwout, dbo

    return jax.shard_map(
        local_block, mesh=mesh,
        in_specs=(tok_spec, tok_spec, P(), P(), P(), P(), P(), P(), P()),
        out_specs=(tok_spec, tok_spec, P(), P(), P(), P(), P(), P()), check_vma=False)
```

time: 293 us -> 245 us (0.84)
  the two profiles are of different devices: /device:TPU:0 before, /device:TPU:3 now
where the time goes in v3:
time: 245 us; the launch traced here: 241 us
  Pallas kernels  235 us (96%)
  local copies, waits for them, and re-layouts  5.84 us (2%)
    pallas_call x1, Pallas kernels, layer_call(): pl.pallas_call(layer_kernel, out_shape=(tok, tok, jax.ShapeDtypeStruct((8...  217 us
    pallas_call x1, Pallas kernels, unpack_call(): pl.pallas_call(unpack_kernel, grid_spec=pltpu.PrefetchScalarGridSpec(num_...  17.4 us

profile of v3, /device:TPU:3, one launch (start us, length us, event | category | flops | bytes accessed | tf_op | source)
XLA Modules:
  0.0 241.4 jit_solution(9114972298864912030)
XLA Ops:
  0.6 1.3 broadcast_in_dim.8.b3_ref
  2.0 217.2 %layer.1 = (bf16[4,128,1024]{2,1,0:T(8,128)(2,1)}, bf16[4,128,1024]{2,1,0:T(8,128)(2,1)}, f32[8,1024]{1,0:T(8,128)}, f32[8,2,520,384]{3,2,1,0:T(8,128)}, f32[2,8,64,1024]{3,2,1,0:T(8,128)}) custom-call(s32[16]{0:T(128)} %kind_ref.3, bf16[4,128,1024]{2,1,0:T(8,128)(2,1)} %x_ref.1, bf16[4,128,1024]{2,1,0:T(8,128)(2,1)} %dy_ref.1, bf16[1024]{0:T(1024)(128)(2,1)} %gamma_ref.1, ...), custom_call_target="tpu_custom_call" | custom-call | tf_op jit(solution)/shard_map/layer/pallas_call | solution.py:592
  219.1 17.4 %unpack.1 = (f32[1024,3072]{1,0:T(8,128)}, f32[3072]{0:T(1024)}, f32[1024,1024]{1,0:T(8,128)}, f32[1024]{0:T(1024)}, f32[1024]{0:T(1024)}, /*index=5*/f32[1024]{0:T(1024)}) custom-call(s32[16]{0:T(128)} %kind_ref.3, f32[8,1040,384]{2,1,0:T(8,128)} %bitcast.4, f32[8,1040,384]{2,1,0:T(8,128)} %bitcast.5, f32[1024,1024]{1,0:T(8,128)} %bitcast.6, ...), custom_call_target="tpu_custom_call" | custom-call | tf_op jit(solution)/shard_map/unpack/pallas_call | solution.py:638
  236.5 2.3 copy.19
  238.8 2.3 copy.20
